TPU v7x, 32 devices: a whole 2x2x4 slice. The times are simulated.
32 devices in a mesh: band: 16 (over z, y, core), spin: 2 (over x).
Axes of the slice: x: 2, y: 2, z: 4, core: 2. Of those that a mesh axis runs over, the one named last changes fastest.
Arguments:
- coefficients: bfloat16 [2, 2, 32, 524288], P('spin', None, 'band'), may hold values from -1 to 1
- occupation: int32 [2, 32], P('spin', 'band'), may hold values from 0 to 1000
- miller: int32 [3, 524288], P(None, ('band', 'spin')), may hold values from -8 to 8
- density: float32 [2, 256, 128, 128], P('spin', 'band'), may hold values from 0.25 to 2
- local_factor: float32 [2, 256, 128, 128], P(None, None, 'band'), may hold values from -1.2 to 1.2
Outputs:
- stress: float32 [6], replicated
- kinetic_density: float32 [524288], P(('band', 'spin'))
- gradient_square: float32 [2, 256, 128, 128], P('spin', 'band')
All inputs are finite; a program needn't handle non-finite values.
Results may differ from a plain program's by a relative error of at most 0.0003.
Values sent between devices are 32-bit elements; how exact they have to be, the bound alone decides.
A program may use at most 64 MiB of HBM per device.

v0:
```python
import functools

import jax
import jax.numpy as jnp
import numpy as np
from jax import lax
from jax.experimental import pallas as pl
from jax.experimental.pallas import tpu as pltpu
from jax.sharding import PartitionSpec as P

occupation_unit = 1000.0
kpoint = (0.25, 0.125, 0.375)
spacing = 0.25
MESH = pl.DeviceIdType.MESH
VMEM = pl.BlockSpec(memory_space=pltpu.VMEM)


def derivative_table(length):
    index = np.arange(length)
    wrapped = np.mod(index[:, None] - index[None, :], length)
    angles = np.pi / length * wrapped
    sines = np.where(wrapped == 0, 1.0, np.sin(angles))
    parity = 1.0 - 2.0 * np.mod(wrapped, 2)
    table = np.where(wrapped == 0, 0.0, 0.5 * parity * np.cos(angles) / sines)
    return table.astype(np.float32)


def fourier_tables(length):
    index = np.arange(length)
    phases = np.mod(index[:, None] * index[None, :], length) * (2.0 * np.pi / length)
    return np.cos(phases), np.sin(phases)


def greet_all(nb, ns):
    b, s = lax.axis_index("band"), lax.axis_index("spin")
    barrier = pltpu.get_barrier_semaphore()

    def greet(k, carry):
        pl.semaphore_signal(
            barrier,
            inc=1,
            device_id=((b + k // ns) % nb, (s + k % ns) % ns),
            device_id_type=MESH,
        )
        return carry

    lax.fori_loop(1, nb * ns, greet, 0)
    pl.semaphore_wait(barrier, nb * ns - 1)
    return b, s


def far_first(k, count):
    return 1 + (k + count // 2 - 1) % (count - 1)


def split(value):
    high = value.astype(jnp.bfloat16)
    return high, (value - high.astype(jnp.float32)).astype(jnp.bfloat16)


def host_split(table):
    high = table.astype(np.float32).astype(jnp.bfloat16)
    low = (table - high.astype(np.float64)).astype(np.float32).astype(jnp.bfloat16)
    return np.stack([high, low])


def dot3(left, right):
    def one(p, q):
        return jnp.dot(p, q, preferred_element_type=jnp.float32)

    return one(left[0], right[0]) + (one(left[0], right[1]) + one(left[1], right[0]))


def loop(low, high, step):
    def body(k, carry):
        step(k)
        return carry

    lax.fori_loop(low, high, body, 0)


def axis_frequency(index, length):
    signed = jnp.where(index >= length // 2, index - length, index)
    return 2.0 * np.pi / length * signed.astype(jnp.float32)


def fold(value):
    return jnp.sum(value, axis=0, keepdims=True)


def main_kernel(
    nb, ns, ny, nz, occupation, dens_h, coef_h, factor_h,
    table_x_h, table_y_h, table_d_h, table_z_h, table_g_h, pairs_h, miller_h,
    stress, kdens, square,
    dens, coef, factor, table_x, table_y, table_d, table_z, table_g, pairs, miller,
    kin, dcol, half, spec, grad, from_core, sum_core, from_plane, sum_plane, from_line,
    scol, gout, grad_x, grad_y, part, held,
    f_sem, d_send, d_recv, h_send, h_recv, c_send, c_recv, p_send, p_recv, l_send, l_recv,
    s_send, s_recv, g_send, g_recv, t_send, t_recv,
):
    sources = (dens_h, coef_h, pairs_h, table_x_h, table_y_h, table_g_h, table_d_h, table_z_h, factor_h, miller_h)
    targets = (dens, coef, pairs, table_x, table_y, table_g, table_d, table_z, factor, miller)
    fetches = [
        pltpu.make_async_copy(source, target, f_sem.at[i])
        for i, (source, target) in enumerate(zip(sources, targets))
    ]
    for fetch in fetches:
        fetch.start()
    b, s = greet_all(nb, ns)
    n = nb * ns
    core, y, z = b % 2, (b // 2) % ny, b // (2 * ny)
    zl, _, xl, width = dens.shape
    zh = zl // ns
    nx = nb * xl
    nzg = nb * zl
    rows = kdens.shape[0]
    fetches[0].wait()

    half_copies = []
    for k in range(1, ns):
        other = (s + k) % ns
        copy = pltpu.make_async_remote_copy(
            dens.at[pl.ds(other * zh, zh)], half.at[k - 1], h_send.at[k - 1], h_recv.at[k - 1],
            device_id=(b, other), device_id_type=MESH,
        )
        copy.start()
        half_copies.append(copy)

    def column_copy(k):
        to = (b + far_first(k, nb)) % nb
        return pltpu.make_async_remote_copy(
            dens.at[:, to], dcol.at[b], d_send.at[k], d_recv.at[k],
            device_id=(to, s), device_id_type=MESH,
        )

    loop(0, nb - 1, lambda k: column_copy(k).start())
    dcol[b] = dens[:, b]

    nbl = occupation.shape[1]
    depth = rows * nbl
    band = lax.broadcasted_iota(jnp.int32, (depth, 128), 0) % nbl
    weight = jnp.zeros((depth, 128), jnp.float32)
    for j in range(nbl):
        share = jnp.full((depth, 128), occupation[0, j]).astype(jnp.float32) / occupation_unit
        weight = jnp.where(band == j, share, weight)
    for fetch in fetches[1:3]:
        fetch.wait()

    def kinetic(i):
        here = pl.ds(pl.multiple_of(i * depth, depth), depth)
        real, imag = coef[0, here, :].astype(jnp.float32), coef[1, here, :].astype(jnp.float32)
        high, low = split(weight * (real * real + imag * imag))
        kin[i // (2 * ns), (i // ns) % 2, i % ns] = jnp.dot(
            pairs[...], high, preferred_element_type=jnp.float32
        ) + jnp.dot(pairs[...], low, preferred_element_type=jnp.float32)

    loop(0, n, kinetic)
    core_copy = pltpu.make_async_remote_copy(
        kin.at[:, 1 - core], from_core, c_send.at[0], c_recv.at[0],
        device_id=(b + 1 - 2 * core, s), device_id_type=MESH,
    )
    core_copy.start()
    core_copy.wait()

    def add_core(i):
        sum_core[i // ny, i % ny] = kin[i, core] + from_core[i]

    loop(0, nz * ny, add_core)
    plane_copies = []
    for k in range(1, ny * ns):
        ty, ts = (y + k // ns) % ny, (s + k % ns) % ns
        copy = pltpu.make_async_remote_copy(
            sum_core.at[:, ty, ts], from_plane.at[k - 1], p_send.at[k - 1], p_recv.at[k - 1],
            device_id=((z * ny + ty) * 2 + core, ts), device_id_type=MESH,
        )
        copy.start()
        plane_copies.append(copy)

    for copy in half_copies:
        copy.wait()
    for fetch in fetches[3:5]:
        fetch.wait()

    def plane(i):
        total = dens[s * zh + i]
        for k in range(ns - 1):
            total = total + half[k, i]
        along = dot3((table_x[0], table_x[1]), split(total.reshape(nx, width)))
        both = split(jnp.concatenate([along[:nx], along[nx:]], axis=1))
        for k in range(ns):
            spec[k, i] = dot3(both, (table_y[0, k], table_y[1, k])).reshape(nb, xl, -1)

    loop(0, zh, plane)

    def spec_copy(k):
        offset = far_first(k, n)
        tb, ts = (b + offset // ns) % nb, (s + offset % ns) % ns
        return pltpu.make_async_remote_copy(
            spec.at[ts, :, tb], scol.at[b, s], s_send.at[k], s_recv.at[k],
            device_id=(tb, ts), device_id_type=MESH,
        )

    loop(0, n - 1, lambda k: spec_copy(k).start())
    scol[b, s] = spec[s, :, b]

    fetches[5].wait()

    def in_plane(i):
        value = split(dens[i].reshape(nx, width))
        grad_x[i] = dot3((table_g[0, 0], table_g[1, 0]), value)
        grad_y[i] = dot3(value, (table_g[0, 1], table_g[1, 1]))

    loop(0, zl, in_plane)

    for copy in plane_copies:
        copy.wait()
    total = sum_core[:, y, s]
    for k in range(1, ny * ns):
        total = total + from_plane[k - 1]
    sum_plane[...] = total

    def line_copy(k):
        tz = (z + k) % nz
        return pltpu.make_async_remote_copy(
            sum_plane.at[tz], from_line.at[k - 1], l_send.at[k - 1], l_recv.at[k - 1],
            device_id=((tz * ny + y) * 2 + core, s), device_id_type=MESH,
        )

    loop(1, nz, lambda k: line_copy(k).start())

    fetches[6].wait()
    loop(0, nb - 1, lambda k: column_copy(k).wait())
    for x in range(xl):
        column = split(dcol[:, :, x, :].reshape(nb * zl, width))
        grad[:, :, x, :] = dot3((table_d[0], table_d[1]), column).reshape(nb, zl, width)

    def grad_copy(k):
        to = (b + far_first(k, nb)) % nb
        return pltpu.make_async_remote_copy(
            grad.at[to], gout.at[:, b], g_send.at[k], g_recv.at[k],
            device_id=(to, s), device_id_type=MESH,
        )

    loop(0, nb - 1, lambda k: grad_copy(k).start())
    gout[:, b] = grad[b]

    loop(1, nz, lambda k: line_copy(k).wait())
    kweight = sum_plane[z] + jnp.sum(from_line[...], axis=0)
    fetches[9].wait()
    gk = [spacing * (miller[i].reshape(rows, 128).astype(jnp.float32) + kpoint[i]) for i in range(3)]
    kdens[...] = 0.5 * (gk[0] * gk[0] + gk[1] * gk[1] + gk[2] * gk[2]) * kweight
    scaled = kweight * (-1.0 / (n * rows * 128))
    order = ((0, 0), (1, 1), (2, 2), (1, 2), (0, 2), (0, 1))
    part[...] = jnp.zeros_like(part)
    for i, (p, q) in enumerate(order):
        part[pl.ds(i, 1), :] = fold(scaled * gk[p] * gk[q])

    loop(0, n - 1, lambda k: spec_copy(k).wait())
    for fetch in fetches[7:9]:
        fetch.wait()
    lanes = scol.shape[4]
    count = lanes // 2
    lane = lax.broadcasted_iota(jnp.int32, (nzg, lanes), 1)
    first = lane < count
    freq_z = axis_frequency(lax.broadcasted_iota(jnp.int32, (nzg, lanes), 0), nzg)
    freq_y = axis_frequency(lane % count + s * count, width)
    row_y = freq_y[:1]
    share = lane * 0 + s
    for x in range(xl):
        column = split(scol[:, :, :, x, :].reshape(nzg, lanes))
        turned = dot3((table_z[0], table_z[1]), column)
        swapped = pltpu.roll(turned[nzg:], count, 1)
        value = turned[:nzg] + jnp.where(first, swapped, -swapped)
        local = jnp.zeros_like(value)
        for k in range(ns):
            left, right = factor[0, :, x, :], factor[1, :, x, :]
            if k > 0:
                left = pltpu.roll(left, width - k * count, 1)
            if k != 1:
                right = pltpu.roll(right, (width - k * count + count) % width, 1)
            local = jnp.where(share == k, jnp.where(first, left, right), local)
        position = jnp.full((nzg, lanes), b * xl + x)
        freq_x = axis_frequency(position, nx)
        length = freq_x * freq_x + freq_y * freq_y + freq_z * freq_z
        positive = length > 0
        inverse = jnp.where(positive, 1.0 / jnp.where(positive, length, 1.0), 0.0)
        hartree = 4.0 * np.pi * value * value * inverse
        weigh = 2.0 * (hartree * inverse + value * local)
        weigh_z = weigh * freq_z
        plain, along_z, along_zz = fold(weigh), fold(weigh_z), fold(weigh_z * freq_z)
        trace = fold(hartree)
        row_x = freq_x[:1]
        terms = (
            plain * row_x * row_x - trace,
            plain * row_y * row_y - trace,
            along_zz - trace,
            along_z * row_y,
            along_z * row_x,
            plain * row_x * row_y,
        )
        for i, term in enumerate(terms):
            part[pl.ds(i, 1), :] += term

    loop(0, nb - 1, lambda k: grad_copy(k).wait())

    def exchange(i):
        value = dens[i].reshape(nx, width)
        g = (grad_x[i], grad_y[i], gout[i].reshape(nx, width))
        total = g[0] * g[0] + g[1] * g[1] + g[2] * g[2]
        square[i] = total
        scale = 4.0 * value * value + 1.0
        weigh = jnp.exp(jnp.log(value) * (-1.0 / 3.0)) * scale / (scale + total)
        weigh = weigh * (-1.0 / (nzg * nx * width))
        for j, (p, q) in enumerate(order):
            part[pl.ds(j, 1), :] += fold(weigh * g[p] * g[q])

    loop(0, zl, exchange)

    def stress_copy(k):
        tb, ts = (b + k // ns) % nb, (s + k % ns) % ns
        return pltpu.make_async_remote_copy(
            part, held.at[k - 1], t_send.at[k - 1], t_recv.at[k - 1],
            device_id=(tb, ts), device_id_type=MESH,
        )

    loop(1, n, lambda k: stress_copy(k).start())
    loop(1, n, lambda k: stress_copy(k).wait())
    stress[...] = part[...] + jnp.sum(held[...], axis=0)


def params(number):
    return pltpu.CompilerParams(
        collective_id=number, has_side_effects=True, vmem_limit_bytes=60 * 2**20
    )


def f32(*shape):
    return jax.ShapeDtypeStruct(shape, jnp.float32)


def shards(nb, ns, coefficients, occupation, miller, density, local_factor):
    dma = pltpu.SemaphoreType.DMA
    _, zl, nx, ny = density.shape
    nzg = zl * nb
    xl = nx // nb
    zh = zl // ns
    part = ny // ns
    lanes = 2 * part
    npw = coefficients.shape[3]
    rows = npw // (nb * ns * 128)
    nbl = coefficients.shape[2]
    fold_y = 2 if nb % 4 == 0 else 1
    fold_z = nb // (2 * fold_y)

    coef = coefficients[0].reshape(2, nbl, npw // 128, 128)
    coef = coef.transpose(0, 2, 1, 3).reshape(2, npw // 128 * nbl, 128)
    pairs = jnp.asarray(np.kron(np.eye(rows), np.ones((1, nbl))), jnp.bfloat16)
    cos_x, sin_x = fourier_tables(nx)
    cos_y, sin_y = fourier_tables(ny)
    cos_z, sin_z = fourier_tables(nzg)
    table_y = []
    for k in range(ns):
        cut = slice(k * part, (k + 1) * part)
        table_y.append(np.block([[cos_y[:, cut], -sin_y[:, cut]], [sin_y[:, cut], cos_y[:, cut]]]))
    in_plane = [derivative_table(nx).astype(np.float64), derivative_table(ny).T.astype(np.float64)]
    fetched = (
        density[0].reshape(zl, nb, xl, ny),
        coef,
        local_factor,
        host_split(np.concatenate([cos_x, -sin_x])),
        host_split(np.stack(table_y)),
        host_split(derivative_table(nzg).astype(np.float64)),
        host_split(np.concatenate([cos_z, sin_z]) / (nzg * nx * ny)),
        host_split(np.stack(in_plane)),
        pairs,
        miller,
    )

    stress, kinetic_density, square = pl.pallas_call(
        functools.partial(main_kernel, nb, ns, fold_y, fold_z),
        out_shape=(f32(8, 128), f32(rows, 128), f32(zl, nx, ny)),
        in_specs=[pl.BlockSpec(memory_space=pltpu.SMEM)]
        + [pl.BlockSpec(memory_space=pltpu.HBM)] * len(fetched),
        out_specs=(VMEM,) * 3,
        scratch_shapes=[pltpu.VMEM(value.shape, value.dtype) for value in fetched]
        + [
            pltpu.VMEM(shape, jnp.float32)
            for shape in (
                (fold_z * fold_y, 2, ns, rows, 128),
                (nb, zl, xl, ny),
                (ns - 1, zh, nb, xl, ny),
                (ns, zh, nb, xl, lanes),
                (nb, zl, xl, ny),
                (fold_z * fold_y, ns, rows, 128),
                (fold_z, fold_y, ns, rows, 128),
                (fold_y * ns - 1, fold_z, rows, 128),
                (fold_z, rows, 128),
                (fold_z - 1, rows, 128),
                (nb, ns, zh, xl, lanes),
                (zl, nb, xl, ny),
                (zl, nx, ny),
                (zl, nx, ny),
                (8, 128),
                (nb * ns - 1, 8, 128),
            )
        ]
        + [dma((len(fetched),))]
        + [
            dma((count,))
            for length in (
                nb - 1, ns - 1, 1, fold_y * ns - 1, fold_z - 1, nb * ns - 1, nb - 1, nb * ns - 1,
            )
            for count in (length, length)
        ],
        compiler_params=params(0),
        name="main_exchange",
    )(occupation, *fetched)
    return (
        jnp.sum(stress[:6], axis=1),
        kinetic_density.reshape(rows * 128),
        square[None],
    )


def solution(mesh):
    return jax.shard_map(
        functools.partial(shards, mesh.shape["band"], mesh.shape["spin"]),
        mesh=mesh,
        in_specs=(
            P("spin", None, "band", None),
            P("spin", "band"),
            P(None, ("band", "spin")),
            P("spin", "band", None, None),
            P(None, None, "band", None),
        ),
        out_specs=(P(), P(("band", "spin")), P("spin", "band", None, None)),
        check_vma=False,
    )
```

profile of v0, /device:TPU:0, one launch (start us, length us, event | category | flops | bytes accessed | tf_op | source)
XLA Modules:
  0.0 97.2 jit_solution(5192153370199564265)
XLA Ops:
  0.6 91.5 %main_exchange.1 = (f32[8,128]{1,0:T(8,128)}, f32[128,128]{1,0:T(8,128)}, f32[16,128,128]{2,1,0:T(8,128)}) custom-call(s32[1,2]{1,0:T(1,128)} %occupation.1, f32[16,16,8,128]{3,2,1,0:T(8,128)} %bitcast.9, bf16[2,8192,128]{2,1,0:T(8,128)(2,1)} %bitcast.8, f32[2,256,8,128]{3,2,1,0:T(8,128)} %factor_h.1, bf16[2,256,128]{2,1,0:T(8,128)(2,1)} %constant.15.clone.table_x_h, ...), custom_call_target="tpu_custom_call" | custom-call | tf_op jit(solution)/shard_map/main_exchange/pallas_call | solution.py:379
  92.1 1.3 %slice_reduce_fusion = f32[6]{0:T(128)} fusion(f32[8,128]{1,0:T(8,128)} %get-tuple-element.6), kind=kLoop, calls=%fused_computation | loop fusion | flops 762 | bytes 3096 | tf_op jit(solution)/shard_map/reduce_sum | solution.py:419
  93.4 1.5 %copy.17 = f32[16384]{0:T(1024)} copy(f32[16384]{0:T(1024)} %bitcast.11) | data formatting | bytes 131072
  94.9 2.3 %copy.18 = f32[1,16,128,128]{3,2,1,0:T(8,128)} copy(f32[1,16,128,128]{3,2,1,0:T(8,128)} %bitcast.10) | data formatting | bytes 2097152
where the time goes:
time: 97.5 us; the launch traced here: 97.2 us
  Pallas kernels  91.5 us (94%)
  local copies, waits for them, and re-layouts  3.77 us (4%)
  other arithmetic  1.3 us (1%)
    pallas_call x1, Pallas kernels, shards(): pl.pallas_call(functools.partial(main_kernel, nb, ns, fold_y, fold_z), ou...  91.5 us
    unnamed x2, local copies, waits for them, and re-layouts  3.77 us

commit v1 on v0

v1 whole, which is shorter than its diff:
```python
import functools

import jax
import jax.numpy as jnp
import numpy as np
from jax import lax
from jax.experimental import pallas as pl
from jax.experimental.pallas import tpu as pltpu
from jax.sharding import PartitionSpec as P

occupation_unit = 1000.0
kpoint = (0.25, 0.125, 0.375)
spacing = 0.25
MESH = pl.DeviceIdType.MESH
VMEM = pl.BlockSpec(memory_space=pltpu.VMEM)
CHUNKS = 2


def derivative_table(length):
    index = np.arange(length)
    wrapped = np.mod(index[:, None] - index[None, :], length)
    angles = np.pi / length * wrapped
    sines = np.where(wrapped == 0, 1.0, np.sin(angles))
    parity = 1.0 - 2.0 * np.mod(wrapped, 2)
    table = np.where(wrapped == 0, 0.0, 0.5 * parity * np.cos(angles) / sines)
    return table.astype(np.float32)


def fourier_tables(length):
    index = np.arange(length)
    phases = np.mod(index[:, None] * index[None, :], length) * (2.0 * np.pi / length)
    return np.cos(phases), np.sin(phases)


def greet_all(nb, ns):
    b, s = lax.axis_index("band"), lax.axis_index("spin")
    barrier = pltpu.get_barrier_semaphore()

    def greet(k, carry):
        pl.semaphore_signal(
            barrier,
            inc=1,
            device_id=((b + k // ns) % nb, (s + k % ns) % ns),
            device_id_type=MESH,
        )
        return carry

    lax.fori_loop(1, nb * ns, greet, 0)
    pl.semaphore_wait(barrier, nb * ns - 1)
    return b, s


def far_first(k, count):
    return 1 + (k + count // 2 - 1) % (count - 1)


def split(value):
    high = value.astype(jnp.bfloat16)
    return high, (value - high.astype(jnp.float32)).astype(jnp.bfloat16)


def host_split(table):
    high = table.astype(np.float32).astype(jnp.bfloat16)
    low = (table - high.astype(np.float64)).astype(np.float32).astype(jnp.bfloat16)
    return np.stack([high, low])


def dot3(left, right):
    def one(p, q):
        return jnp.dot(p, q, preferred_element_type=jnp.float32)

    return one(left[0], right[0]) + (one(left[0], right[1]) + one(left[1], right[0]))


def loop(low, high, step):
    def body(k, carry):
        step(k)
        return carry

    lax.fori_loop(low, high, body, 0)


def axis_frequency(index, length):
    signed = jnp.where(index >= length // 2, index - length, index)
    return 2.0 * np.pi / length * signed.astype(jnp.float32)


def fold(value):
    return jnp.sum(value, axis=0, keepdims=True)


def guard(always, condition, step):
    if always:
        step()
    else:
        pl.when(condition)(step)


def stack3(left, right):
    high, low = right
    depth = high.shape[0]
    return jnp.dot(
        left, jnp.concatenate([high, high], axis=0), preferred_element_type=jnp.float32
    ) + jnp.dot(left[:, :depth], low, preferred_element_type=jnp.float32)


def main_kernel(
    nb, ns, ny, nz, occupation, dens_h, coef_h, factor_h,
    table_f_h, table_i_h, table_y_h, table_d_h, table_z_h, table_g_h, pairs_h, miller_h,
    stress, kdens, square,
    dens, coef, factor, table_f, table_i, table_y, table_d, table_z, table_g, pairs, miller,
    kin, out, col, grad, gout, from_core, sum_core, from_plane, sum_plane, from_line,
    inverses, grad_x, grad_y, part, row, held,
    f_sem, d_send, d_recv, c_send, c_recv, p_send, p_recv, l_send, l_recv,
    g_send, g_recv, t_send, t_recv,
):
    sources = (dens_h, table_f_h, coef_h, pairs_h, table_g_h, table_d_h, table_y_h, table_z_h, factor_h, table_i_h, miller_h)
    targets = (dens, table_f, coef, pairs, table_g, table_d, table_y, table_z, factor, table_i, miller)
    fetches = [
        pltpu.make_async_copy(source, target, f_sem.at[i])
        for i, (source, target) in enumerate(zip(sources, targets))
    ]
    for fetch in fetches:
        fetch.start()
    b, s = greet_all(nb, ns)
    n = nb * ns
    core, y, z = b % 2, (b // 2) % ny, b // (2 * ny)
    zl, nx, width = dens.shape
    chunks, _, _, block, _ = col.shape
    hb = nb // 2
    half, u = b // hb, b % hb
    xl = nx // nb
    na = min(ns, xl)
    per = xl // na
    each = per // chunks
    rc = 2 * each
    zp = block // rc
    hz = hb * zl
    nzg = nb * zl
    rows = kdens.shape[0]
    whole, mine = na == ns, s < na
    for fetch in fetches[:2]:
        fetch.wait()

    def peer(k, count):
        offset = far_first(k, count * ns)
        return (offset // ns, (s + offset % ns) % ns)

    def block_copy(c, k):
        step, ts = peer(k, nb)
        tb = (b + step) % nb
        at = pl.multiple_of((tb * na + ts) * block, block)
        return ts < na, pltpu.make_async_remote_copy(
            out.at[c, pl.ds(at, block), :], col.at[c, s, b], d_send.at[c, k], d_recv.at[c, k],
            device_id=(tb, ts), device_id_type=MESH,
        )

    for c in range(chunks):

        def forward(i):
            value = split(jnp.concatenate([dens[2 * i], dens[2 * i + 1]], axis=1))
            turned = stack3(table_f[c], value)
            out[c, pl.ds(2 * i, nb * na * rc, stride=zp), :] = turned[:, :width]
            out[c, pl.ds(2 * i + 1, nb * na * rc, stride=zp), :] = turned[:, width:]

        loop(0, zl // 2, forward)

        def send(k):
            right, copy = block_copy(c, k)
            guard(whole, right, copy.start)

        loop(0, n - 1, send)

        def keep():
            at = pl.multiple_of((b * na + s) * block, block)
            col[c, s, b] = out[c, pl.ds(at, block), :]

        guard(whole, mine, keep)

    nbl = occupation.shape[1]
    depth = rows * nbl
    band = lax.broadcasted_iota(jnp.int32, (depth, 128), 0) % nbl
    weight = jnp.zeros((depth, 128), jnp.float32)
    for j in range(nbl):
        share = jnp.full((depth, 128), occupation[0, j]).astype(jnp.float32) / occupation_unit
        weight = jnp.where(band == j, share, weight)
    for fetch in fetches[2:4]:
        fetch.wait()

    def kinetic(i):
        here = pl.ds(pl.multiple_of(i * depth, depth), depth)
        real, imag = coef[0, here, :].astype(jnp.float32), coef[1, here, :].astype(jnp.float32)
        high, low = split(weight * (real * real + imag * imag))
        kin[i // (2 * ns), (i // ns) % 2, i % ns] = jnp.dot(
            pairs[...], high, preferred_element_type=jnp.float32
        ) + jnp.dot(pairs[...], low, preferred_element_type=jnp.float32)

    loop(0, n, kinetic)
    core_copy = pltpu.make_async_remote_copy(
        kin.at[:, 1 - core], from_core, c_send.at[0], c_recv.at[0],
        device_id=(b + 1 - 2 * core, s), device_id_type=MESH,
    )
    core_copy.start()

    fetches[4].wait()

    def in_plane(i):
        value = split(dens[i])
        grad_x[i] = dot3((table_g[0, 0], table_g[1, 0]), value)
        grad_y[i] = dot3(value, (table_g[0, 1], table_g[1, 1]))

    loop(0, zl, in_plane)

    core_copy.wait()

    def add_core(i):
        sum_core[i // ny, i % ny] = kin[i, core] + from_core[i]

    loop(0, nz * ny, add_core)
    plane_copies = []
    for k in range(1, ny * ns):
        ty, ts = (y + k // ns) % ny, (s + k % ns) % ns
        copy = pltpu.make_async_remote_copy(
            sum_core.at[:, ty, ts], from_plane.at[k - 1], p_send.at[k - 1], p_recv.at[k - 1],
            device_id=((z * ny + ty) * 2 + core, ts), device_id_type=MESH,
        )
        copy.start()
        plane_copies.append(copy)

    freq_z = axis_frequency(lax.broadcasted_iota(jnp.int32, (nzg, width), 0), nzg)
    freq_y = axis_frequency(lax.broadcasted_iota(jnp.int32, (nzg, width), 1), width)
    row_y = freq_y[:1]

    def place(j):
        return b * xl + s * per + j

    def invert(j):
        freq_x = axis_frequency(jnp.full((nzg, width), place(j)), nx)
        length = freq_x * freq_x + freq_y * freq_y + freq_z * freq_z
        positive = length > 0
        inverses[j] = jnp.where(positive, 1.0 / jnp.where(positive, length, 1.0), 0.0)

    loop(0, per, invert)

    for copy in plane_copies:
        copy.wait()
    total = sum_core[:, y, s]
    for k in range(1, ny * ns):
        total = total + from_plane[k - 1]
    sum_plane[...] = total

    def line_copy(k):
        tz = (z + k) % nz
        return pltpu.make_async_remote_copy(
            sum_plane.at[tz], from_line.at[k - 1], l_send.at[k - 1], l_recv.at[k - 1],
            device_id=((tz * ny + y) * 2 + core, s), device_id_type=MESH,
        )

    loop(1, nz, lambda k: line_copy(k).start())
    part[...] = jnp.zeros_like(part)
    for fetch in fetches[5:10]:
        fetch.wait()

    def back_copy(c, k):
        step, ts = peer(k, hb)
        tu = (u + step) % hb
        at = pl.multiple_of(((c * hb + u) * na + s) * block, block)
        return (s - (ts - s)) % ns < na, pltpu.make_async_remote_copy(
            grad.at[c, ts, tu], gout.at[pl.ds(at, block), :], g_send.at[c, k], g_recv.at[c, k],
            device_id=(half * hb + tu, ts), device_id_type=MESH,
        )

    def column(c, k, r):
        return col[c, k, :, pl.ds(pl.multiple_of(r * zp, zp), zl), :].reshape(nzg, width)

    rows_d = pl.ds(pl.multiple_of(half * hz, hz), hz)
    for c in range(chunks):

        def receive(k):
            right, copy = block_copy(c, k)
            guard(whole, right, copy.wait_send)
            guard(whole, mine, copy.wait_recv)

        loop(0, n - 1, receive)

        def derive(j):
            k, r = j // each, 2 * (j % each)
            value = split(jnp.concatenate([column(c, k, r), column(c, k, r + 1)], axis=1))
            slope = dot3((table_d[0, rows_d, :], table_d[1, rows_d, :]), value)
            for i in range(2):
                here = pl.ds(pl.multiple_of((r + i) * zp, zp), zl)
                grad[c, k, :, here, :] = slope[:, i * width:(i + 1) * width].reshape(hb, zl, width)

        def give_back(k):
            back_copy(c, k)[1].start()

        def local_back():
            at = pl.multiple_of(((c * hb + u) * na + s) * block, block)
            gout[pl.ds(at, block), :] = grad[c, s, u]

        def transform(i):
            j = c * each + i
            real, imag = column(c, 0, i), column(c, 0, each + i)
            for k in range(1, ns):
                real, imag = real + column(c, k, i), imag + column(c, k, each + i)
            position = jnp.full((nzg, width), place(j))
            imag = jnp.where(position % (nx // 2) == 0, 0.0, imag)
            value = split(jnp.concatenate([real, imag], axis=1))
            value = split(dot3(value, (table_y[0], table_y[1])))
            turned = dot3((table_z[0], table_z[1]), value)
            real = turned[:nzg, :width] + turned[nzg:, width:]
            imag = turned[:nzg, width:] - turned[nzg:, :width]
            inverse = inverses[j]
            here = s * per + j
            local = real * factor[0, :, here, :] + imag * factor[1, :, here, :]
            hartree = (4.0 * np.pi) * (real * real + imag * imag) * inverse
            weigh = 2.0 * (hartree * inverse + local)
            weigh_z = weigh * freq_z
            plain, along_z, along_zz = fold(weigh), fold(weigh_z), fold(weigh_z * freq_z)
            trace = fold(hartree)
            row_x = axis_frequency(position[:1], nx)
            terms = (
                plain * row_x * row_x - trace,
                plain * row_y * row_y - trace,
                along_zz - trace,
                along_z * row_y,
                along_z * row_x,
                plain * row_x * row_y,
            )
            for i, term in enumerate(terms):
                part[pl.ds(i, 1), :] += term

        def work():
            loop(0, ns * each, derive)
            loop(0, hb * ns - 1, give_back)
            local_back()
            loop(0, each, transform)

        guard(whole, mine, work)

    loop(1, nz, lambda k: line_copy(k).wait())
    kweight = sum_plane[z] + jnp.sum(from_line[...], axis=0)
    fetches[10].wait()
    gk = [spacing * (miller[i].reshape(rows, 128).astype(jnp.float32) + kpoint[i]) for i in range(3)]
    kdens[...] = 0.5 * (gk[0] * gk[0] + gk[1] * gk[1] + gk[2] * gk[2]) * kweight
    scaled = kweight * (-1.0 / (n * rows * 128))
    order = ((0, 0), (1, 1), (2, 2), (1, 2), (0, 2), (0, 1))
    for i, (p, q) in enumerate(order):
        part[pl.ds(i, 1), :] += fold(scaled * gk[p] * gk[q])

    for c in range(chunks):

        def collect(k):
            right, copy = back_copy(c, k)
            guard(whole, mine, copy.wait_send)
            guard(whole, right, copy.wait_recv)

        loop(0, hb * ns - 1, collect)

    def exchange(i):
        slope = jnp.concatenate(
            [gout[pl.ds(2 * i + j, nx, stride=zp), :] for j in range(2)], axis=1
        )
        slope = stack3(table_i[half], split(slope))
        for j in range(2):
            value = dens[2 * i + j]
            g = (grad_x[2 * i + j], grad_y[2 * i + j], slope[:, j * width:(j + 1) * width])
            total = g[0] * g[0] + g[1] * g[1] + g[2] * g[2]
            square[2 * i + j] = total
            scale = 4.0 * value * value + 1.0
            weigh = jnp.exp(jnp.log(value) * (-1.0 / 3.0)) * scale / (scale + total)
            weigh = weigh * (-1.0 / (nzg * nx * width))
            for t, (p, q) in enumerate(order):
                part[pl.ds(t, 1), :] += fold(weigh * g[p] * g[q])

    loop(0, zl // 2, exchange)
    spots = [lax.broadcasted_iota(jnp.int32, (8, 128), i) for i in range(2)]
    sums = jnp.sum(part[...], axis=1, keepdims=True)
    row[...] = fold(jnp.where(spots[0] == spots[1], sums, 0.0))

    def stress_copy(k):
        tb, ts = (b + k // ns) % nb, (s + k % ns) % ns
        return pltpu.make_async_remote_copy(
            row, held.at[k - 1], t_send.at[k - 1], t_recv.at[k - 1],
            device_id=(tb, ts), device_id_type=MESH,
        )

    loop(1, n, lambda k: stress_copy(k).start())
    loop(1, n, lambda k: stress_copy(k).wait())
    stress[...] = row[...] + jnp.sum(held[...], axis=0)


def params(number):
    return pltpu.CompilerParams(
        collective_id=number, has_side_effects=True, vmem_limit_bytes=60 * 2**20
    )


def f32(*shape):
    return jax.ShapeDtypeStruct(shape, jnp.float32)


def real_basis(nb, na, chunks, nx):
    xl = nx // nb
    per = xl // na
    each = per // chunks
    x = np.arange(nx)
    basis = np.zeros((chunks, nb, na, 2, each, nx))
    share = np.zeros((chunks, nb, na, 2, each))
    for b in range(nb):
        for j in range(xl):
            k = b * xl + j
            phases = (2.0 * np.pi / nx) * ((k * x) % nx)
            spot = (j % per // each, b, j // per, slice(None), j % each)
            if k % (nx // 2) == 0:
                other = (2.0 * np.pi / nx) * (((nx // 2 - k) * x) % nx)
                basis[spot] = np.stack([np.cos(phases), np.cos(other)])
                share[spot] = 1.0 / nx
            else:
                basis[spot] = np.stack([np.cos(phases), -np.sin(phases)])
                share[spot] = 2.0 / nx
    inverse = (basis * share[..., None]).reshape(chunks, 2, nb // 2, -1, nx)
    inverse = inverse.transpose(1, 4, 0, 2, 3).reshape(2, nx, nx)
    return basis.reshape(chunks, -1, nx), inverse


def beside(table):
    return np.concatenate(list(host_split(table)), axis=-1)


def shards(nb, ns, coefficients, occupation, miller, density, local_factor):
    dma = pltpu.SemaphoreType.DMA
    _, zl, nx, ny = density.shape
    nzg = zl * nb
    xl = nx // nb
    na = min(ns, xl)
    per = xl // na
    chunks = min(CHUNKS, per)
    rc = 2 * (per // chunks)
    zp = zl
    while rc * zp % 8:
        zp += 1
    block = rc * zp
    npw = coefficients.shape[3]
    rows = npw // (nb * ns * 128)
    nbl = coefficients.shape[2]
    fold_y = 2 if nb % 4 == 0 else 1
    fold_z = nb // (2 * fold_y)
    hb = nb // 2

    coef = coefficients[0].reshape(2, nbl, npw // 128, 128)
    coef = coef.transpose(0, 2, 1, 3).reshape(2, npw // 128 * nbl, 128)
    pairs = jnp.asarray(np.kron(np.eye(rows), np.ones((1, nbl))), jnp.bfloat16)
    basis, inverse = real_basis(nb, na, chunks, nx)
    cos_y, sin_y = fourier_tables(ny)
    cos_z, sin_z = fourier_tables(nzg)
    table_y = np.block([[cos_y, -sin_y], [sin_y, cos_y]])
    in_plane = [derivative_table(nx).astype(np.float64), derivative_table(ny).T.astype(np.float64)]
    fetched = (
        density[0],
        coef,
        local_factor,
        beside(basis),
        beside(inverse),
        host_split(table_y),
        host_split(derivative_table(nzg).astype(np.float64)),
        host_split(np.concatenate([cos_z, sin_z]) / (nzg * nx * ny)),
        host_split(np.stack(in_plane)),
        pairs,
        miller,
    )

    stress, kinetic_density, square = pl.pallas_call(
        functools.partial(main_kernel, nb, ns, fold_y, fold_z),
        out_shape=(f32(1, 128), f32(rows, 128), f32(zl, nx, ny)),
        in_specs=[pl.BlockSpec(memory_space=pltpu.SMEM)]
        + [pl.BlockSpec(memory_space=pltpu.HBM)] * len(fetched),
        out_specs=(VMEM,) * 3,
        scratch_shapes=[pltpu.VMEM(value.shape, value.dtype) for value in fetched]
        + [
            pltpu.VMEM(shape, jnp.float32)
            for shape in (
                (fold_z * fold_y, 2, ns, rows, 128),
                (chunks, nb * na * block, ny),
                (chunks, ns, nb, block, ny),
                (chunks, ns, hb, block, ny),
                (chunks * hb * na * block, ny),
                (fold_z * fold_y, ns, rows, 128),
                (fold_z, fold_y, ns, rows, 128),
                (fold_y * ns - 1, fold_z, rows, 128),
                (fold_z, rows, 128),
                (fold_z - 1, rows, 128),
                (per, nzg, ny),
                (zl, nx, ny),
                (zl, nx, ny),
                (8, 128),
                (1, 128),
                (nb * ns - 1, 1, 128),
            )
        ]
        + [dma((len(fetched),))]
        + [
            dma(shape)
            for shape in (
                (chunks, nb * ns - 1), (1,), (fold_y * ns - 1,), (fold_z - 1,),
                (chunks, hb * ns - 1), (nb * ns - 1,),
            )
            for _ in range(2)
        ],
        compiler_params=params(0),
        name="main_exchange",
    )(occupation, *fetched)
    return (
        stress[0, :6],
        kinetic_density.reshape(rows * 128),
        square[None],
    )


def solution(mesh):
    return jax.shard_map(
        functools.partial(shards, mesh.shape["band"], mesh.shape["spin"]),
        mesh=mesh,
        in_specs=(
            P("spin", None, "band", None),
            P("spin", "band"),
            P(None, ("band", "spin")),
            P("spin", "band", None, None),
            P(None, None, "band", None),
        ),
        out_specs=(P(), P(("band", "spin")), P("spin", "band", None, None)),
        check_vma=False,
    )
```

time: 97.5 us -> 84.5 us (0.87)
  Pallas kernels: 91.5 us -> 78.7 us
  other arithmetic: 1.3 us -> 0 us
  local copies, waits for them, and re-layouts: 3.77 us -> 4.94 us
    pallas_call x1, Pallas kernels: 91.5 us -> 78.7 us  [shards(): pl.pallas_call(functools.partial(main_kernel, nb, ns, fold_y, fold_z), ou...]
    reduce_sum x1 -> x0, other arithmetic: 1.3 us -> none  [shards(): jnp.sum(stress[:6], axis=1)]
    squeeze x0 -> x1, local copies, waits for them, and re-layouts: none -> 1.18 us  [shards(): return (stress[0, :6], kinetic_density.reshape(rows * 128), square[None])]
where the time goes in v1:
time: 84.5 us; the launch traced here: 84.3 us
  Pallas kernels  78.7 us (93%)
  local copies, waits for them, and re-layouts  4.94 us (6%)
    pallas_call x1, Pallas kernels, shards(): pl.pallas_call(functools.partial(main_kernel, nb, ns, fold_y, fold_z), ou...  78.7 us
    unnamed x2, local copies, waits for them, and re-layouts  3.77 us

profile of v1, /device:TPU:0, one launch (start us, length us, event | category | flops | bytes accessed | tf_op | source)
XLA Modules:
  0.0 84.3 jit_solution(1134014740745962304)
XLA Ops:
  0.6 78.7 %main_exchange.1 = (f32[1,128]{1,0:T(1,128)}, f32[128,128]{1,0:T(8,128)}, f32[16,128,128]{2,1,0:T(8,128)}) custom-call(s32[1,2]{1,0:T(1,128)} %occupation.1, f32[16,128,128]{2,1,0:T(8,128)} %bitcast.11, bf16[2,8192,128]{2,1,0:T(8,128)(2,1)} %bitcast.10, f32[2,256,8,128]{3,2,1,0:T(8,128)} %factor_h.1, bf16[2,128,256]{2,1,0:T(8,128)(2,1)} %constant.15.clone.table_f_h, ...), custom_call_target="tpu_custom_call" | custom-call | tf_op jit(solution)/shard_map/main_exchange/pallas_call | solution.py:473
  79.4 1.2 %slice_bitcast_fusion = f32[6]{0:T(128)} fusion(f32[1,128]{1,0:T(1,128)} %get-tuple-element.6), kind=kLoop, calls=%fused_computation | loop fusion | bytes 48 | tf_op jit(solution)/shard_map/squeeze | solution.py:514
  80.5 1.5 %copy.18 = f32[16384]{0:T(1024)} copy(f32[16384]{0:T(1024)} %bitcast.13) | data formatting | bytes 131072
  82.0 2.3 %copy.19 = f32[1,16,128,128]{3,2,1,0:T(8,128)} copy(f32[1,16,128,128]{3,2,1,0:T(8,128)} %bitcast.12) | data formatting | bytes 2097152

commit v2 on v1

--- a/solution.py
+++ b/solution.py
@@ -13,7 +13,7 @@
 spacing = 0.25
 MESH = pl.DeviceIdType.MESH
 VMEM = pl.BlockSpec(memory_space=pltpu.VMEM)
-CHUNKS = 2
+CHUNKS = 4
 
 
 def derivative_table(length):
@@ -36,17 +36,16 @@
     b, s = lax.axis_index("band"), lax.axis_index("spin")
     barrier = pltpu.get_barrier_semaphore()
 
-    def greet(k, carry):
+    def greet(k):
+        offset = far_first(k, nb * ns)
         pl.semaphore_signal(
             barrier,
             inc=1,
-            device_id=((b + k // ns) % nb, (s + k % ns) % ns),
+            device_id=((b + offset // ns) % nb, (s + offset % ns) % ns),
             device_id_type=MESH,
         )
-        return carry
-
-    lax.fori_loop(1, nb * ns, greet, 0)
-    pl.semaphore_wait(barrier, nb * ns - 1)
+
+    loop(0, nb * ns - 1, greet)
     return b, s
 
 
@@ -110,7 +109,7 @@
     stress, kdens, square,
     dens, coef, factor, table_f, table_i, table_y, table_d, table_z, table_g, pairs, miller,
     kin, out, col, grad, gout, from_core, sum_core, from_plane, sum_plane, from_line,
-    inverses, grad_x, grad_y, part, row, held,
+    inverses, grad_x, grad_y, above, slopes, tally, part, row, held,
     f_sem, d_send, d_recv, c_send, c_recv, p_send, p_recv, l_send, l_recv,
     g_send, g_recv, t_send, t_recv,
 ):
@@ -120,7 +119,7 @@
         pltpu.make_async_copy(source, target, f_sem.at[i])
         for i, (source, target) in enumerate(zip(sources, targets))
     ]
-    for fetch in fetches:
+    for fetch in fetches[:2]:
         fetch.start()
     b, s = greet_all(nb, ns)
     n = nb * ns
@@ -141,6 +140,8 @@
     whole, mine = na == ns, s < na
     for fetch in fetches[:2]:
         fetch.wait()
+    for fetch in fetches[2:]:
+        fetch.start()
 
     def peer(k, count):
         offset = far_first(k, count * ns)
@@ -155,16 +156,14 @@
             device_id=(tb, ts), device_id_type=MESH,
         )
 
-    for c in range(chunks):
-
-        def forward(i):
-            value = split(jnp.concatenate([dens[2 * i], dens[2 * i + 1]], axis=1))
+    def forward(i, which):
+        value = split(jnp.concatenate([dens[2 * i], dens[2 * i + 1]], axis=1))
+        for c in which:
             turned = stack3(table_f[c], value)
             out[c, pl.ds(2 * i, nb * na * rc, stride=zp), :] = turned[:, :width]
             out[c, pl.ds(2 * i + 1, nb * na * rc, stride=zp), :] = turned[:, width:]
 
-        loop(0, zl // 2, forward)
-
+    def send_chunk(c):
         def send(k):
             right, copy = block_copy(c, k)
             guard(whole, right, copy.start)
@@ -176,6 +175,20 @@
             col[c, s, b] = out[c, pl.ds(at, block), :]
 
         guard(whole, mine, keep)
+
+    def forward_first(i):
+        forward(i, range(1))
+
+    def forward_rest(i):
+        forward(i, range(1, chunks))
+
+    loop(0, zl // 2, forward_first)
+    pl.semaphore_wait(pltpu.get_barrier_semaphore(), n - 1)
+    send_chunk(0)
+    if chunks > 1:
+        loop(0, zl // 2, forward_rest)
+    for c in range(1, chunks):
+        send_chunk(c)
 
     nbl = occupation.shape[1]
     depth = rows * nbl
@@ -208,6 +221,9 @@
         value = split(dens[i])
         grad_x[i] = dot3((table_g[0, 0], table_g[1, 0]), value)
         grad_y[i] = dot3(value, (table_g[0, 1], table_g[1, 1]))
+        scale = 4.0 * dens[i] * dens[i] + 1.0
+        weigh = jnp.exp(jnp.log(dens[i]) * (-1.0 / 3.0)) * scale
+        above[i] = weigh * (-1.0 / (nzg * nx * width))
 
     loop(0, zl, in_plane)
 
@@ -242,22 +258,8 @@
 
     loop(0, per, invert)
 
-    for copy in plane_copies:
-        copy.wait()
-    total = sum_core[:, y, s]
-    for k in range(1, ny * ns):
-        total = total + from_plane[k - 1]
-    sum_plane[...] = total
-
-    def line_copy(k):
-        tz = (z + k) % nz
-        return pltpu.make_async_remote_copy(
-            sum_plane.at[tz], from_line.at[k - 1], l_send.at[k - 1], l_recv.at[k - 1],
-            device_id=((tz * ny + y) * 2 + core, s), device_id_type=MESH,
-        )
-
-    loop(1, nz, lambda k: line_copy(k).start())
     part[...] = jnp.zeros_like(part)
+    tally[...] = jnp.zeros_like(tally)
     for fetch in fetches[5:10]:
         fetch.wait()
 
@@ -272,6 +274,52 @@
 
     def column(c, k, r):
         return col[c, k, :, pl.ds(pl.multiple_of(r * zp, zp), zl), :].reshape(nzg, width)
+
+    def line_copy(k):
+        tz = (z + k) % nz
+        return pltpu.make_async_remote_copy(
+            sum_plane.at[tz], from_line.at[k - 1], l_send.at[k - 1], l_recv.at[k - 1],
+            device_id=((tz * ny + y) * 2 + core, s), device_id_type=MESH,
+        )
+
+    def finish_planes():
+        for copy in plane_copies:
+            copy.wait()
+        total = sum_core[:, y, s]
+        for k in range(1, ny * ns):
+            total = total + from_plane[k - 1]
+        sum_plane[...] = total
+        loop(1, nz, lambda k: line_copy(k).start())
+
+    def gather_back(c):
+        def collect(k):
+            right, copy = back_copy(c, k)
+            guard(whole, mine, copy.wait_send)
+            guard(whole, right, copy.wait_recv)
+
+        loop(0, hb * ns - 1, collect)
+
+    def returned(c, i):
+        count = hb * na * rc
+        high, low = split(
+            jnp.concatenate(
+                [
+                    gout[pl.ds(c * count * zp + 2 * i + j, count, stride=zp), :]
+                    for j in range(2)
+                ],
+                axis=1,
+            )
+        )
+        return jnp.dot(
+            table_i[half, c], jnp.concatenate([high, low, high], axis=0),
+            preferred_element_type=jnp.float32,
+        )
+
+    def invert_chunk(c, i):
+        value = returned(c, i)
+        for j in range(2):
+            here = value[:, j * width:(j + 1) * width]
+            slopes[2 * i + j] = here if c == 0 else slopes[2 * i + j] + here
 
     rows_d = pl.ds(pl.multiple_of(half * hz, hz), hz)
     for c in range(chunks):
@@ -337,6 +385,11 @@
             loop(0, each, transform)
 
         guard(whole, mine, work)
+        if c == max(chunks - 2, 0):
+            finish_planes()
+        if c > 0:
+            gather_back(c - 1)
+            loop(0, zl // 2, functools.partial(invert_chunk, c - 1))
 
     loop(1, nz, lambda k: line_copy(k).wait())
     kweight = sum_plane[z] + jnp.sum(from_line[...], axis=0)
@@ -348,45 +401,49 @@
     for i, (p, q) in enumerate(order):
         part[pl.ds(i, 1), :] += fold(scaled * gk[p] * gk[q])
 
-    for c in range(chunks):
-
-        def collect(k):
-            right, copy = back_copy(c, k)
-            guard(whole, mine, copy.wait_send)
-            guard(whole, right, copy.wait_recv)
-
-        loop(0, hb * ns - 1, collect)
+    gather_back(chunks - 1)
 
     def exchange(i):
-        slope = jnp.concatenate(
-            [gout[pl.ds(2 * i + j, nx, stride=zp), :] for j in range(2)], axis=1
-        )
-        slope = stack3(table_i[half], split(slope))
+        last = returned(chunks - 1, i)
+        tallies = [tally[t] for t in range(len(order))]
         for j in range(2):
-            value = dens[2 * i + j]
-            g = (grad_x[2 * i + j], grad_y[2 * i + j], slope[:, j * width:(j + 1) * width])
+            here = last[:, j * width:(j + 1) * width]
+            if chunks > 1:
+                here = here + slopes[2 * i + j]
+            g = (grad_x[2 * i + j], grad_y[2 * i + j], here)
             total = g[0] * g[0] + g[1] * g[1] + g[2] * g[2]
             square[2 * i + j] = total
-            scale = 4.0 * value * value + 1.0
-            weigh = jnp.exp(jnp.log(value) * (-1.0 / 3.0)) * scale / (scale + total)
-            weigh = weigh * (-1.0 / (nzg * nx * width))
+            value = dens[2 * i + j]
+            weigh = above[2 * i + j] / (4.0 * value * value + 1.0 + total)
+            scaled = [weigh * g[p] for p in range(3)]
             for t, (p, q) in enumerate(order):
-                part[pl.ds(t, 1), :] += fold(weigh * g[p] * g[q])
+                term = (scaled[p] * g[q]).reshape(nx // 8, 8, width)
+                tallies[t] = tallies[t] + jnp.sum(term, axis=0)
+        for t in range(len(order)):
+            tally[t] = tallies[t]
 
     loop(0, zl // 2, exchange)
+    for t in range(len(order)):
+        part[pl.ds(t, 1), :] += fold(tally[t])
     spots = [lax.broadcasted_iota(jnp.int32, (8, 128), i) for i in range(2)]
     sums = jnp.sum(part[...], axis=1, keepdims=True)
     row[...] = fold(jnp.where(spots[0] == spots[1], sums, 0.0))
 
     def stress_copy(k):
-        tb, ts = (b + k // ns) % nb, (s + k % ns) % ns
+        step, ts = peer(k, nb)
         return pltpu.make_async_remote_copy(
-            row, held.at[k - 1], t_send.at[k - 1], t_recv.at[k - 1],
-            device_id=(tb, ts), device_id_type=MESH,
-        )
-
-    loop(1, n, lambda k: stress_copy(k).start())
-    loop(1, n, lambda k: stress_copy(k).wait())
+            row, held.at[k], t_send.at[k], t_recv.at[k],
+            device_id=((b + step) % nb, ts), device_id_type=MESH,
+        )
+
+    def share_stress(k):
+        stress_copy(k).start()
+
+    def wait_stress(k):
+        stress_copy(k).wait()
+
+    loop(0, n - 1, share_stress)
+    loop(0, n - 1, wait_stress)
     stress[...] = row[...] + jnp.sum(held[...], axis=0)
 
 
@@ -419,8 +476,8 @@
             else:
                 basis[spot] = np.stack([np.cos(phases), -np.sin(phases)])
                 share[spot] = 2.0 / nx
-    inverse = (basis * share[..., None]).reshape(chunks, 2, nb // 2, -1, nx)
-    inverse = inverse.transpose(1, 4, 0, 2, 3).reshape(2, nx, nx)
+    inverse = (basis * share[..., None]).reshape(chunks, 2, -1, nx)
+    inverse = inverse.transpose(1, 0, 3, 2)
     return basis.reshape(chunks, -1, nx), inverse
 
 
@@ -461,7 +518,7 @@
         coef,
         local_factor,
         beside(basis),
-        beside(inverse),
+        np.concatenate([host_split(inverse)[k] for k in (0, 0, 1)], axis=-1),
         host_split(table_y),
         host_split(derivative_table(nzg).astype(np.float64)),
         host_split(np.concatenate([cos_z, sin_z]) / (nzg * nx * ny)),
@@ -493,6 +550,9 @@
                 (per, nzg, ny),
                 (zl, nx, ny),
                 (zl, nx, ny),
+                (zl, nx, ny),
+                (zl, nx, ny),
+                (6, 8, ny),
                 (8, 128),
                 (1, 128),
                 (nb * ns - 1, 1, 128),

time: 84.5 us -> 83.3 us (0.986)
  Pallas kernels: 78.7 us -> 77.5 us
    pallas_call x1, Pallas kernels: 78.7 us -> 77.5 us  [shards(): pl.pallas_call(functools.partial(main_kernel, nb, ns, fold_y, fold_z), ou...]
where the time goes in v2:
time: 83.3 us; the launch traced here: 83.1 us
  Pallas kernels  77.5 us (93%)
  local copies, waits for them, and re-layouts  4.94 us (6%)
    pallas_call x1, Pallas kernels, shards(): pl.pallas_call(functools.partial(main_kernel, nb, ns, fold_y, fold_z), ou...  77.5 us
    unnamed x2, local copies, waits for them, and re-layouts  3.77 us

profile of v2, /device:TPU:0, one launch (start us, length us, event | category | flops | bytes accessed | tf_op | source)
XLA Modules:
  0.0 83.1 jit_solution(6442028666365301520)
XLA Ops:
  0.6 77.5 %main_exchange.1 = (f32[1,128]{1,0:T(1,128)}, f32[128,128]{1,0:T(8,128)}, f32[16,128,128]{2,1,0:T(8,128)}) custom-call(s32[1,2]{1,0:T(1,128)} %occupation.1, f32[16,128,128]{2,1,0:T(8,128)} %bitcast.11, bf16[2,8192,128]{2,1,0:T(8,128)(2,1)} %bitcast.10, f32[2,256,8,128]{3,2,1,0:T(8,128)} %factor_h.1, bf16[4,64,256]{2,1,0:T(8,128)(2,1)} %constant.15.clone.table_f_h, ...), custom_call_target="tpu_custom_call" | custom-call | tf_op jit(solution)/shard_map/main_exchange/pallas_call | solution.py:530
  78.2 1.2 %slice_bitcast_fusion = f32[6]{0:T(128)} fusion(f32[1,128]{1,0:T(1,128)} %get-tuple-element.6), kind=kLoop, calls=%fused_computation | loop fusion | bytes 48 | tf_op jit(solution)/shard_map/squeeze | solution.py:574
  79.3 1.5 %copy.18 = f32[16384]{0:T(1024)} copy(f32[16384]{0:T(1024)} %bitcast.13) | data formatting | bytes 131072
  80.8 2.3 %copy.19 = f32[1,16,128,128]{3,2,1,0:T(8,128)} copy(f32[1,16,128,128]{3,2,1,0:T(8,128)} %bitcast.12) | data formatting | bytes 2097152

commit v3 on v2

--- a/solution.py
+++ b/solution.py
@@ -12,8 +12,8 @@
 kpoint = (0.25, 0.125, 0.375)
 spacing = 0.25
 MESH = pl.DeviceIdType.MESH
-VMEM = pl.BlockSpec(memory_space=pltpu.VMEM)
 CHUNKS = 4
+AHEAD = 2
 
 
 def derivative_table(length):
@@ -32,25 +32,31 @@
     return np.cos(phases), np.sin(phases)
 
 
+def wrapped(value, count):
+    return jnp.where(value >= count, value - count, value)
+
+
+def far_first(count, step):
+    loop(count // 2, count, step)
+    loop(1, count // 2, step)
+
+
+def partner(b, s, offset, nb, ns):
+    hop = lax.div(offset, ns)
+    return wrapped(b + hop, nb), wrapped(s + offset - hop * ns, ns)
+
+
 def greet_all(nb, ns):
     b, s = lax.axis_index("band"), lax.axis_index("spin")
     barrier = pltpu.get_barrier_semaphore()
 
     def greet(k):
-        offset = far_first(k, nb * ns)
         pl.semaphore_signal(
-            barrier,
-            inc=1,
-            device_id=((b + offset // ns) % nb, (s + offset % ns) % ns),
-            device_id_type=MESH,
-        )
-
-    loop(0, nb * ns - 1, greet)
+            barrier, inc=1, device_id=partner(b, s, k, nb, ns), device_id_type=MESH
+        )
+
+    far_first(nb * ns, greet)
     return b, s
-
-
-def far_first(k, count):
-    return 1 + (k + count // 2 - 1) % (count - 1)
 
 
 def split(value):
@@ -103,18 +109,22 @@
     ) + jnp.dot(left[:, :depth], low, preferred_element_type=jnp.float32)
 
 
+def settle(ref, semaphore):
+    pltpu.make_async_copy(ref, ref, semaphore).wait()
+
+
 def main_kernel(
     nb, ns, ny, nz, occupation, dens_h, coef_h, factor_h,
-    table_f_h, table_i_h, table_y_h, table_d_h, table_z_h, table_g_h, pairs_h, miller_h,
-    stress, kdens, square,
-    dens, coef, factor, table_f, table_i, table_y, table_d, table_z, table_g, pairs, miller,
-    kin, out, col, grad, gout, from_core, sum_core, from_plane, sum_plane, from_line,
+    table_f_h, table_i_h, table_y_h, table_d_h, table_z_h, table_g_h, miller_h,
+    stress_o, kdens_o, square_o,
+    dens, coef, factor, table_f, table_i, table_y, table_d, table_z, table_g, miller,
+    stress, kdens, square, squares, kin, out, col, grad, gout, from_core, sum_core, from_plane, sum_plane, from_line, pair, from_pair,
     inverses, grad_x, grad_y, above, slopes, tally, part, row, held,
-    f_sem, d_send, d_recv, c_send, c_recv, p_send, p_recv, l_send, l_recv,
+    f_sem, o_sem, d_send, d_recv, c_send, c_recv, p_send, p_recv, l_send, l_recv, x_send, x_recv,
     g_send, g_recv, t_send, t_recv,
 ):
-    sources = (dens_h, table_f_h, coef_h, pairs_h, table_g_h, table_d_h, table_y_h, table_z_h, factor_h, table_i_h, miller_h)
-    targets = (dens, table_f, coef, pairs, table_g, table_d, table_y, table_z, factor, table_i, miller)
+    sources = (dens_h, table_f_h, coef_h, table_g_h, table_d_h, table_y_h, table_z_h, factor_h, table_i_h, miller_h)
+    targets = (dens, table_f, coef, table_g, table_d, table_y, table_z, factor, table_i, miller)
     fetches = [
         pltpu.make_async_copy(source, target, f_sem.at[i])
         for i, (source, target) in enumerate(zip(sources, targets))
@@ -143,16 +153,11 @@
     for fetch in fetches[2:]:
         fetch.start()
 
-    def peer(k, count):
-        offset = far_first(k, count * ns)
-        return (offset // ns, (s + offset % ns) % ns)
-
     def block_copy(c, k):
-        step, ts = peer(k, nb)
-        tb = (b + step) % nb
+        tb, ts = partner(b, s, k, nb, ns)
         at = pl.multiple_of((tb * na + ts) * block, block)
         return ts < na, pltpu.make_async_remote_copy(
-            out.at[c, pl.ds(at, block), :], col.at[c, s, b], d_send.at[c, k], d_recv.at[c, k],
+            out.at[c, pl.ds(at, block), :], col.at[c, s, b], d_send.at[c], d_recv.at[c],
             device_id=(tb, ts), device_id_type=MESH,
         )
 
@@ -168,11 +173,11 @@
             right, copy = block_copy(c, k)
             guard(whole, right, copy.start)
 
-        loop(0, n - 1, send)
+        far_first(n, send)
 
         def keep():
             at = pl.multiple_of((b * na + s) * block, block)
-            col[c, s, b] = out[c, pl.ds(at, block), :]
+            pltpu.make_async_copy(out.at[c, pl.ds(at, block), :], col.at[c, s, b], d_recv.at[c]).start()
 
         guard(whole, mine, keep)
 
@@ -185,37 +190,53 @@
     loop(0, zl // 2, forward_first)
     pl.semaphore_wait(pltpu.get_barrier_semaphore(), n - 1)
     send_chunk(0)
-    if chunks > 1:
-        loop(0, zl // 2, forward_rest)
-    for c in range(1, chunks):
-        send_chunk(c)
 
     nbl = occupation.shape[1]
     depth = rows * nbl
-    band = lax.broadcasted_iota(jnp.int32, (depth, 128), 0) % nbl
-    weight = jnp.zeros((depth, 128), jnp.float32)
-    for j in range(nbl):
-        share = jnp.full((depth, 128), occupation[0, j]).astype(jnp.float32) / occupation_unit
-        weight = jnp.where(band == j, share, weight)
-    for fetch in fetches[2:4]:
-        fetch.wait()
+    shares = [
+        jnp.full((rows, 128), occupation[0, j]).astype(jnp.float32) / occupation_unit
+        for j in range(nbl)
+    ]
+    fetches[2].wait()
 
     def kinetic(i):
-        here = pl.ds(pl.multiple_of(i * depth, depth), depth)
-        real, imag = coef[0, here, :].astype(jnp.float32), coef[1, here, :].astype(jnp.float32)
-        high, low = split(weight * (real * real + imag * imag))
-        kin[i // (2 * ns), (i // ns) % 2, i % ns] = jnp.dot(
-            pairs[...], high, preferred_element_type=jnp.float32
-        ) + jnp.dot(pairs[...], low, preferred_element_type=jnp.float32)
-
-    loop(0, n, kinetic)
+        for j in range(2):
+            k = 2 * i + j
+            here = pl.ds(pl.multiple_of(k * depth, depth), depth)
+            real, imag = coef[0, here, :].astype(jnp.float32), coef[1, here, :].astype(jnp.float32)
+            squares[j] = real * real + imag * imag
+            total = shares[0] * squares[j, pl.ds(0, rows, stride=nbl), :]
+            for m in range(1, nbl):
+                total = total + shares[m] * squares[j, pl.ds(m, rows, stride=nbl), :]
+            kin[lax.div(k, 2 * ns), lax.rem(lax.div(k, ns), 2), lax.rem(k, ns)] = total
+
+    loop(0, n // 2, kinetic)
     core_copy = pltpu.make_async_remote_copy(
         kin.at[:, 1 - core], from_core, c_send.at[0], c_recv.at[0],
         device_id=(b + 1 - 2 * core, s), device_id_type=MESH,
     )
     core_copy.start()
-
-    fetches[4].wait()
+    if chunks > 1:
+        loop(0, zl // 2, forward_rest)
+    core_copy.wait()
+
+    def add_core(i):
+        sum_core[lax.div(i, ny), lax.rem(i, ny)] = kin[i, core] + from_core[i]
+
+    loop(0, nz * ny, add_core)
+    plane_copies = []
+    for k in range(1, ny * ns):
+        ty, ts = (y + k // ns) % ny, (s + k % ns) % ns
+        copy = pltpu.make_async_remote_copy(
+            sum_core.at[:, ty, ts], from_plane.at[k - 1], p_send.at[k - 1], p_recv.at[k - 1],
+            device_id=((z * ny + ty) * 2 + core, ts), device_id_type=MESH,
+        )
+        copy.start()
+        plane_copies.append(copy)
+    for c in range(1, min(AHEAD, chunks)):
+        send_chunk(c)
+
+    fetches[3].wait()
 
     def in_plane(i):
         value = split(dens[i])
@@ -227,22 +248,6 @@
 
     loop(0, zl, in_plane)
 
-    core_copy.wait()
-
-    def add_core(i):
-        sum_core[i // ny, i % ny] = kin[i, core] + from_core[i]
-
-    loop(0, nz * ny, add_core)
-    plane_copies = []
-    for k in range(1, ny * ns):
-        ty, ts = (y + k // ns) % ny, (s + k % ns) % ns
-        copy = pltpu.make_async_remote_copy(
-            sum_core.at[:, ty, ts], from_plane.at[k - 1], p_send.at[k - 1], p_recv.at[k - 1],
-            device_id=((z * ny + ty) * 2 + core, ts), device_id_type=MESH,
-        )
-        copy.start()
-        plane_copies.append(copy)
-
     freq_z = axis_frequency(lax.broadcasted_iota(jnp.int32, (nzg, width), 0), nzg)
     freq_y = axis_frequency(lax.broadcasted_iota(jnp.int32, (nzg, width), 1), width)
     row_y = freq_y[:1]
@@ -260,27 +265,34 @@
 
     part[...] = jnp.zeros_like(part)
     tally[...] = jnp.zeros_like(tally)
-    for fetch in fetches[5:10]:
+    for fetch in fetches[4:9]:
         fetch.wait()
 
     def back_copy(c, k):
-        step, ts = peer(k, hb)
-        tu = (u + step) % hb
+        tu, ts = partner(u, s, k, hb, ns)
         at = pl.multiple_of(((c * hb + u) * na + s) * block, block)
-        return (s - (ts - s)) % ns < na, pltpu.make_async_remote_copy(
-            grad.at[c, ts, tu], gout.at[pl.ds(at, block), :], g_send.at[c, k], g_recv.at[c, k],
+        return wrapped(2 * s - ts + ns, ns) < na, pltpu.make_async_remote_copy(
+            grad.at[c, ts, tu], gout.at[pl.ds(at, block), :], g_send.at[c], g_recv.at[c],
             device_id=(half * hb + tu, ts), device_id_type=MESH,
         )
 
     def column(c, k, r):
         return col[c, k, :, pl.ds(pl.multiple_of(r * zp, zp), zl), :].reshape(nzg, width)
 
+    nh = nz // 2
+    zhalf, zin = z // nh, z % nh
+
     def line_copy(k):
-        tz = (z + k) % nz
+        tz = (zin + k) % nh
         return pltpu.make_async_remote_copy(
-            sum_plane.at[tz], from_line.at[k - 1], l_send.at[k - 1], l_recv.at[k - 1],
-            device_id=((tz * ny + y) * 2 + core, s), device_id_type=MESH,
-        )
+            sum_plane.at[:, tz], from_line.at[k - 1], l_send.at[k - 1], l_recv.at[k - 1],
+            device_id=(((zhalf * nh + tz) * ny + y) * 2 + core, s), device_id_type=MESH,
+        )
+
+    cross_copy = pltpu.make_async_remote_copy(
+        pair.at[1 - zhalf], from_pair, x_send.at[0], x_recv.at[0],
+        device_id=((((1 - zhalf) * nh + zin) * ny + y) * 2 + core, s), device_id_type=MESH,
+    )
 
     def finish_planes():
         for copy in plane_copies:
@@ -288,16 +300,17 @@
         total = sum_core[:, y, s]
         for k in range(1, ny * ns):
             total = total + from_plane[k - 1]
-        sum_plane[...] = total
-        loop(1, nz, lambda k: line_copy(k).start())
+        sum_plane[...] = total.reshape(2, nh, rows, 128)
+        loop(1, nh, lambda k: line_copy(k).start())
+
+    def cross_lines():
+        loop(1, nh, lambda k: line_copy(k).wait())
+        pair[...] = sum_plane[:, zin] + jnp.sum(from_line[...], axis=0)
+        cross_copy.start()
 
     def gather_back(c):
-        def collect(k):
-            right, copy = back_copy(c, k)
-            guard(whole, mine, copy.wait_send)
-            guard(whole, right, copy.wait_recv)
-
-        loop(0, hb * ns - 1, collect)
+        count = hb * na * block
+        settle(gout.at[pl.ds(c * count, count), :], g_recv.at[c])
 
     def returned(c, i):
         count = hb * na * rc
@@ -324,12 +337,7 @@
     rows_d = pl.ds(pl.multiple_of(half * hz, hz), hz)
     for c in range(chunks):
 
-        def receive(k):
-            right, copy = block_copy(c, k)
-            guard(whole, right, copy.wait_send)
-            guard(whole, mine, copy.wait_recv)
-
-        loop(0, n - 1, receive)
+        guard(whole, mine, functools.partial(settle, col.at[c], d_recv.at[c]))
 
         def derive(j):
             k, r = j // each, 2 * (j % each)
@@ -344,7 +352,7 @@
 
         def local_back():
             at = pl.multiple_of(((c * hb + u) * na + s) * block, block)
-            gout[pl.ds(at, block), :] = grad[c, s, u]
+            pltpu.make_async_copy(grad.at[c, s, u], gout.at[pl.ds(at, block), :], g_recv.at[c]).start()
 
         def transform(i):
             j = c * each + i
@@ -380,20 +388,27 @@
 
         def work():
             loop(0, ns * each, derive)
-            loop(0, hb * ns - 1, give_back)
+            far_first(hb * ns, give_back)
             local_back()
+
+        def spectrum():
             loop(0, each, transform)
 
         guard(whole, mine, work)
+        if c + AHEAD < chunks:
+            send_chunk(c + AHEAD)
+        guard(whole, mine, spectrum)
+        if c == max(chunks - 3, 0):
+            finish_planes()
         if c == max(chunks - 2, 0):
-            finish_planes()
+            cross_lines()
         if c > 0:
             gather_back(c - 1)
             loop(0, zl // 2, functools.partial(invert_chunk, c - 1))
 
-    loop(1, nz, lambda k: line_copy(k).wait())
-    kweight = sum_plane[z] + jnp.sum(from_line[...], axis=0)
-    fetches[10].wait()
+    cross_copy.wait()
+    kweight = pair[zhalf] + from_pair[...]
+    fetches[9].wait()
     gk = [spacing * (miller[i].reshape(rows, 128).astype(jnp.float32) + kpoint[i]) for i in range(3)]
     kdens[...] = 0.5 * (gk[0] * gk[0] + gk[1] * gk[1] + gk[2] * gk[2]) * kweight
     scaled = kweight * (-1.0 / (n * rows * 128))
@@ -403,18 +418,21 @@
 
     gather_back(chunks - 1)
 
+    group = 2 if zl % 4 == 0 else 1
+
     def exchange(i):
-        last = returned(chunks - 1, i)
+        lasts = [returned(chunks - 1, group * i + m) for m in range(group)]
         tallies = [tally[t] for t in range(len(order))]
-        for j in range(2):
-            here = last[:, j * width:(j + 1) * width]
+        for j in range(2 * group):
+            spot = 2 * group * i + j
+            here = lasts[j // 2][:, j % 2 * width:(j % 2 + 1) * width]
             if chunks > 1:
-                here = here + slopes[2 * i + j]
-            g = (grad_x[2 * i + j], grad_y[2 * i + j], here)
+                here = here + slopes[spot]
+            g = (grad_x[spot], grad_y[spot], here)
             total = g[0] * g[0] + g[1] * g[1] + g[2] * g[2]
-            square[2 * i + j] = total
-            value = dens[2 * i + j]
-            weigh = above[2 * i + j] / (4.0 * value * value + 1.0 + total)
+            square[spot] = total
+            value = dens[spot]
+            weigh = above[spot] / (4.0 * value * value + 1.0 + total)
             scaled = [weigh * g[p] for p in range(3)]
             for t, (p, q) in enumerate(order):
                 term = (scaled[p] * g[q]).reshape(nx // 8, 8, width)
@@ -422,7 +440,7 @@
         for t in range(len(order)):
             tally[t] = tallies[t]
 
-    loop(0, zl // 2, exchange)
+    loop(0, zl // (2 * group), exchange)
     for t in range(len(order)):
         part[pl.ds(t, 1), :] += fold(tally[t])
     spots = [lax.broadcasted_iota(jnp.int32, (8, 128), i) for i in range(2)]
@@ -430,21 +448,37 @@
     row[...] = fold(jnp.where(spots[0] == spots[1], sums, 0.0))
 
     def stress_copy(k):
-        step, ts = peer(k, nb)
         return pltpu.make_async_remote_copy(
-            row, held.at[k], t_send.at[k], t_recv.at[k],
-            device_id=((b + step) % nb, ts), device_id_type=MESH,
+            row, held.at[k - 1], t_send.at[0], t_recv.at[0],
+            device_id=partner(b, s, k, nb, ns), device_id_type=MESH,
         )
 
     def share_stress(k):
         stress_copy(k).start()
 
-    def wait_stress(k):
-        stress_copy(k).wait()
-
-    loop(0, n - 1, share_stress)
-    loop(0, n - 1, wait_stress)
+    def drain(c, count, semaphore):
+        settle(out.at[c, pl.ds(0, count * block), :], semaphore.at[c])
+
+    results = [
+        pltpu.make_async_copy(value, target, o_sem.at[i])
+        for i, (value, target) in enumerate(
+            ((stress, stress_o), (kdens, kdens_o), (square, square_o))
+        )
+    ]
+    far_first(n, share_stress)
+    for result in results[1:]:
+        result.start()
+    for c in range(chunks):
+        guard(whole, mine, functools.partial(drain, c, nb * na - 1, d_send))
+        guard(whole, mine, functools.partial(drain, c, hb * ns - 1, g_send))
+        if not whole:
+            pl.when(s >= na)(functools.partial(drain, c, nb * na, d_send))
+    settle(held, t_send.at[0])
+    settle(held, t_recv.at[0])
     stress[...] = row[...] + jnp.sum(held[...], axis=0)
+    results[0].start()
+    for result in results:
+        result.wait()
 
 
 def params(number):
@@ -453,8 +487,8 @@
     )
 
 
-def f32(*shape):
-    return jax.ShapeDtypeStruct(shape, jnp.float32)
+def vmem(*shape):
+    return pltpu.VMEM(shape, jnp.float32)
 
 
 def real_basis(nb, na, chunks, nx):
@@ -507,7 +541,6 @@
 
     coef = coefficients[0].reshape(2, nbl, npw // 128, 128)
     coef = coef.transpose(0, 2, 1, 3).reshape(2, npw // 128 * nbl, 128)
-    pairs = jnp.asarray(np.kron(np.eye(rows), np.ones((1, nbl))), jnp.bfloat16)
     basis, inverse = real_basis(nb, na, chunks, nx)
     cos_y, sin_y = fourier_tables(ny)
     cos_z, sin_z = fourier_tables(nzg)
@@ -523,20 +556,23 @@
         host_split(derivative_table(nzg).astype(np.float64)),
         host_split(np.concatenate([cos_z, sin_z]) / (nzg * nx * ny)),
         host_split(np.stack(in_plane)),
-        pairs,
         miller,
     )
 
     stress, kinetic_density, square = pl.pallas_call(
         functools.partial(main_kernel, nb, ns, fold_y, fold_z),
-        out_shape=(f32(1, 128), f32(rows, 128), f32(zl, nx, ny)),
+        out_shape=(vmem(1, 128), vmem(rows, 128), vmem(zl, nx, ny)),
         in_specs=[pl.BlockSpec(memory_space=pltpu.SMEM)]
         + [pl.BlockSpec(memory_space=pltpu.HBM)] * len(fetched),
-        out_specs=(VMEM,) * 3,
+        out_specs=(pl.BlockSpec(memory_space=pl.ANY),) * 3,
         scratch_shapes=[pltpu.VMEM(value.shape, value.dtype) for value in fetched]
         + [
             pltpu.VMEM(shape, jnp.float32)
             for shape in (
+                (1, 128),
+                (rows, 128),
+                (zl, nx, ny),
+                (2, rows * nbl, 128),
                 (fold_z * fold_y, 2, ns, rows, 128),
                 (chunks, nb * na * block, ny),
                 (chunks, ns, nb, block, ny),
@@ -545,8 +581,10 @@
                 (fold_z * fold_y, ns, rows, 128),
                 (fold_z, fold_y, ns, rows, 128),
                 (fold_y * ns - 1, fold_z, rows, 128),
-                (fold_z, rows, 128),
-                (fold_z - 1, rows, 128),
+                (2, fold_z // 2, rows, 128),
+                (fold_z // 2 - 1, 2, rows, 128),
+                (2, rows, 128),
+                (rows, 128),
                 (per, nzg, ny),
                 (zl, nx, ny),
                 (zl, nx, ny),
@@ -558,12 +596,12 @@
                 (nb * ns - 1, 1, 128),
             )
         ]
-        + [dma((len(fetched),))]
+        + [dma((len(fetched),)), dma((3,))]
         + [
             dma(shape)
             for shape in (
-                (chunks, nb * ns - 1), (1,), (fold_y * ns - 1,), (fold_z - 1,),
-                (chunks, hb * ns - 1), (nb * ns - 1,),
+                (chunks,), (1,), (fold_y * ns - 1,), (fold_z // 2 - 1,), (1,),
+                (chunks,), (1,),
             )
             for _ in range(2)
         ],

time: 83.3 us -> 73.5 us (0.88)
  Pallas kernels: 77.5 us -> 70.5 us
  local copies, waits for them, and re-layouts: 4.94 us -> 2.12 us
    pallas_call x1, Pallas kernels: 77.5 us -> 70.5 us  [shards(): pl.pallas_call(functools.partial(main_kernel, nb, ns, fold_y, fold_z), ou...]
    unnamed x2, local copies, waits for them, and re-layouts: 3.77 us -> 1.6 us
where the time goes in v3:
time: 73.5 us; the launch traced here: 73.3 us
  Pallas kernels  70.5 us (96%)
  local copies, waits for them, and re-layouts  2.12 us (3%)
    pallas_call x1, Pallas kernels, shards(): pl.pallas_call(functools.partial(main_kernel, nb, ns, fold_y, fold_z), ou...  70.5 us
    unnamed x2, local copies, waits for them, and re-layouts  1.6 us

profile of v3, /device:TPU:0, one launch (start us, length us, event | category | flops | bytes accessed | tf_op | source)
XLA Modules:
  0.0 73.3 jit_solution(17993854819292102553)
XLA Ops:
  0.6 70.5 %main_exchange.1 = (f32[1,128]{1,0:T(1,128)S(1)}, f32[128,128]{1,0:T(8,128)S(1)}, f32[16,128,128]{2,1,0:T(8,128)S(1)}) custom-call(s32[1,2]{1,0:T(1,128)} %occupation.1, f32[16,128,128]{2,1,0:T(8,128)} %bitcast.13, bf16[2,8192,128]{2,1,0:T(8,128)(2,1)} %bitcast.12, f32[2,256,8,128]{3,2,1,0:T(8,128)} %factor_h.1, ...), custom_call_target="tpu_custom_call" | custom-call | tf_op jit(solution)/shard_map/main_exchange/pallas_call | solution.py:562
  71.2 0.5 slice_bitcast_fusion
  71.7 0.6 copy.17
  72.3 1.0 %copy.18 = f32[1,16,128,128]{3,2,1,0:T(8,128)} copy(f32[1,16,128,128]{3,2,1,0:T(8,128)S(1)} %bitcast.10) | data formatting | bytes 2097152

commit v4 on v3

--- a/solution.py
+++ b/solution.py
@@ -13,7 +13,7 @@
 spacing = 0.25
 MESH = pl.DeviceIdType.MESH
 CHUNKS = 4
-AHEAD = 2
+PLAN = (((0, 0), (1, 0)), ((0, 1), (0, 2), (0, 3), (0, 4), (1, 1), (1, 2)), ((1, 3), (1, 4)))
 
 
 def derivative_table(length):
@@ -129,9 +129,9 @@
         pltpu.make_async_copy(source, target, f_sem.at[i])
         for i, (source, target) in enumerate(zip(sources, targets))
     ]
+    b, s = greet_all(nb, ns)
     for fetch in fetches[:2]:
         fetch.start()
-    b, s = greet_all(nb, ns)
     n = nb * ns
     core, y, z = b % 2, (b // 2) % ny, b // (2 * ny)
     zl, nx, width = dens.shape
@@ -144,6 +144,12 @@
     each = per // chunks
     rc = 2 * each
     zp = block // rc
+    units = [(c, 0, rc) for c in range(chunks - 1)]
+    units += [(chunks - 1, 0, each), (chunks - 1, each, each)]
+    backs = [(m, c, r * zp, count * zp) for m, (c, r, count) in enumerate(units)]
+    if zl % 16 == 0 and each == 1:
+        m, c, edge, _ = backs.pop()
+        backs += [(m, c, edge, zl // 2), (m, c, edge + zl // 2, zl // 2)]
     hz = hb * zl
     nzg = nb * zl
     rows = kdens.shape[0]
@@ -153,12 +159,14 @@
     for fetch in fetches[2:]:
         fetch.start()
 
-    def block_copy(c, k):
-        tb, ts = partner(b, s, k, nb, ns)
-        at = pl.multiple_of((tb * na + ts) * block, block)
+    def block_copy(m, k, cross):
+        c, r, count = units[m]
+        tu, ts = partner(u, s, k, hb, ns)
+        tb = tu + hb * (1 - half if cross else half)
+        at = pl.multiple_of((tb * na + ts) * block + r * zp, 8)
         return ts < na, pltpu.make_async_remote_copy(
-            out.at[c, pl.ds(at, block), :], col.at[c, s, b], d_send.at[c], d_recv.at[c],
-            device_id=(tb, ts), device_id_type=MESH,
+            out.at[c, pl.ds(at, count * zp), :], col.at[c, s, b, pl.ds(r * zp, count * zp), :],
+            d_send.at[m], d_recv.at[m], device_id=(tb, ts), device_id_type=MESH,
         )
 
     def forward(i, which):
@@ -168,18 +176,28 @@
             out[c, pl.ds(2 * i, nb * na * rc, stride=zp), :] = turned[:, :width]
             out[c, pl.ds(2 * i + 1, nb * na * rc, stride=zp), :] = turned[:, width:]
 
-    def send_chunk(c):
+    def send_part(m, cross):
         def send(k):
-            right, copy = block_copy(c, k)
+            right, copy = block_copy(m, k, cross)
             guard(whole, right, copy.start)
 
-        far_first(n, send)
-
-        def keep():
-            at = pl.multiple_of((b * na + s) * block, block)
-            pltpu.make_async_copy(out.at[c, pl.ds(at, block), :], col.at[c, s, b], d_recv.at[c]).start()
-
-        guard(whole, mine, keep)
+        if cross:
+            loop(0, hb * ns, send)
+        else:
+            far_first(hb * ns, send)
+
+    def send_stage(stage):
+        for cross, m in PLAN[stage] if stage < len(PLAN) else ():
+            if m < len(units):
+                send_part(m, cross)
+
+    def keep(m):
+        c, r, count = units[m]
+        at = pl.multiple_of((b * na + s) * block + r * zp, 8)
+        pltpu.make_async_copy(
+            out.at[c, pl.ds(at, count * zp), :], col.at[c, s, b, pl.ds(r * zp, count * zp), :],
+            d_recv.at[m],
+        ).start()
 
     def forward_first(i):
         forward(i, range(1))
@@ -189,7 +207,7 @@
 
     loop(0, zl // 2, forward_first)
     pl.semaphore_wait(pltpu.get_barrier_semaphore(), n - 1)
-    send_chunk(0)
+    send_stage(0)
 
     nbl = occupation.shape[1]
     depth = rows * nbl
@@ -233,8 +251,9 @@
         )
         copy.start()
         plane_copies.append(copy)
-    for c in range(1, min(AHEAD, chunks)):
-        send_chunk(c)
+    send_stage(1)
+    for m in range(len(units)):
+        guard(whole, mine, functools.partial(keep, m))
 
     fetches[3].wait()
 
@@ -268,13 +287,21 @@
     for fetch in fetches[4:9]:
         fetch.wait()
 
-    def back_copy(c, k):
+    def back_copy(i, k):
+        _, c, edge, count = backs[i]
         tu, ts = partner(u, s, k, hb, ns)
-        at = pl.multiple_of(((c * hb + u) * na + s) * block, block)
-        return wrapped(2 * s - ts + ns, ns) < na, pltpu.make_async_remote_copy(
-            grad.at[c, ts, tu], gout.at[pl.ds(at, block), :], g_send.at[c], g_recv.at[c],
-            device_id=(half * hb + tu, ts), device_id_type=MESH,
-        )
+        at = pl.multiple_of(((c * hb + u) * na + s) * block + edge, 8)
+        return pltpu.make_async_remote_copy(
+            grad.at[c, ts, tu, pl.ds(edge, count), :], gout.at[pl.ds(at, count), :],
+            g_send.at[i], g_recv.at[i], device_id=(half * hb + tu, ts), device_id_type=MESH,
+        )
+
+    def local_back(i):
+        _, c, edge, count = backs[i]
+        at = pl.multiple_of(((c * hb + u) * na + s) * block + edge, 8)
+        pltpu.make_async_copy(
+            grad.at[c, s, u, pl.ds(edge, count), :], gout.at[pl.ds(at, count), :], g_recv.at[i]
+        ).start()
 
     def column(c, k, r):
         return col[c, k, :, pl.ds(pl.multiple_of(r * zp, zp), zl), :].reshape(nzg, width)
@@ -308,9 +335,8 @@
         pair[...] = sum_plane[:, zin] + jnp.sum(from_line[...], axis=0)
         cross_copy.start()
 
-    def gather_back(c):
-        count = hb * na * block
-        settle(gout.at[pl.ds(c * count, count), :], g_recv.at[c])
+    def gather_back(i):
+        settle(gout.at[pl.ds(0, hb * na * backs[i][3]), :], g_recv.at[i])
 
     def returned(c, i):
         count = hb * na * rc
@@ -335,24 +361,25 @@
             slopes[2 * i + j] = here if c == 0 else slopes[2 * i + j] + here
 
     rows_d = pl.ds(pl.multiple_of(half * hz, hz), hz)
-    for c in range(chunks):
-
-        guard(whole, mine, functools.partial(settle, col.at[c], d_recv.at[c]))
-
-        def derive(j):
-            k, r = j // each, 2 * (j % each)
+    for m, (c, start, count) in enumerate(units):
+        here = col.at[c, :, :, pl.ds(start * zp, count * zp), :]
+        guard(whole, mine, functools.partial(settle, here, d_recv.at[m]))
+
+        def derive_pair(j):
+            k, r = lax.div(j, each), 2 * lax.rem(j, each)
             value = split(jnp.concatenate([column(c, k, r), column(c, k, r + 1)], axis=1))
             slope = dot3((table_d[0, rows_d, :], table_d[1, rows_d, :]), value)
             for i in range(2):
-                here = pl.ds(pl.multiple_of((r + i) * zp, zp), zl)
-                grad[c, k, :, here, :] = slope[:, i * width:(i + 1) * width].reshape(hb, zl, width)
-
-        def give_back(k):
-            back_copy(c, k)[1].start()
-
-        def local_back():
-            at = pl.multiple_of(((c * hb + u) * na + s) * block, block)
-            pltpu.make_async_copy(grad.at[c, s, u], gout.at[pl.ds(at, block), :], g_recv.at[c]).start()
+                spot = pl.ds(pl.multiple_of((r + i) * zp, zp), zl)
+                grad[c, k, :, spot, :] = slope[:, i * width:(i + 1) * width].reshape(hb, zl, width)
+
+        def derive_spins(j):
+            r = start + j
+            value = split(jnp.concatenate([column(c, k, r) for k in range(ns)], axis=1))
+            slope = dot3((table_d[0, rows_d, :], table_d[1, rows_d, :]), value)
+            for k in range(ns):
+                spot = pl.ds(pl.multiple_of(r * zp, zp), zl)
+                grad[c, k, :, spot, :] = slope[:, k * width:(k + 1) * width].reshape(hb, zl, width)
 
         def transform(i):
             j = c * each + i
@@ -387,24 +414,30 @@
                 part[pl.ds(i, 1), :] += term
 
         def work():
-            loop(0, ns * each, derive)
-            far_first(hb * ns, give_back)
-            local_back()
+            if count == rc:
+                loop(0, ns * each, derive_pair)
+            else:
+                loop(0, count, derive_spins)
+            for i in range(len(backs)):
+                if backs[i][0] == m:
+                    far_first(hb * ns, lambda k: back_copy(i, k).start())
+                    local_back(i)
 
         def spectrum():
             loop(0, each, transform)
 
         guard(whole, mine, work)
-        if c + AHEAD < chunks:
-            send_chunk(c + AHEAD)
-        guard(whole, mine, spectrum)
-        if c == max(chunks - 3, 0):
+        if m == max(chunks - 3, 0):
             finish_planes()
-        if c == max(chunks - 2, 0):
+        send_stage(m + 2)
+        if start + count == rc:
+            guard(whole, mine, spectrum)
+        if m == max(chunks - 2, 0):
             cross_lines()
-        if c > 0:
-            gather_back(c - 1)
-            loop(0, zl // 2, functools.partial(invert_chunk, c - 1))
+        done = m - 2 if start else m - 1
+        if 0 <= done and m != chunks - 1:
+            gather_back(done)
+            loop(0, zl // 2, functools.partial(invert_chunk, done))
 
     cross_copy.wait()
     kweight = pair[zhalf] + from_pair[...]
@@ -415,8 +448,6 @@
     order = ((0, 0), (1, 1), (2, 2), (1, 2), (0, 2), (0, 1))
     for i, (p, q) in enumerate(order):
         part[pl.ds(i, 1), :] += fold(scaled * gk[p] * gk[q])
-
-    gather_back(chunks - 1)
 
     group = 2 if zl % 4 == 0 else 1
 
@@ -440,7 +471,14 @@
         for t in range(len(order)):
             tally[t] = tallies[t]
 
-    loop(0, zl // (2 * group), exchange)
+    steps = zl // (2 * group)
+    late = len(backs) - len(units)
+    for i in range(chunks - 1, len(backs) - late):
+        gather_back(i)
+    loop(0, steps // (1 + late), exchange)
+    if late:
+        gather_back(len(backs) - 1)
+        loop(steps // 2, steps, exchange)
     for t in range(len(order)):
         part[pl.ds(t, 1), :] += fold(tally[t])
     spots = [lax.broadcasted_iota(jnp.int32, (8, 128), i) for i in range(2)]
@@ -457,7 +495,7 @@
         stress_copy(k).start()
 
     def drain(c, count, semaphore):
-        settle(out.at[c, pl.ds(0, count * block), :], semaphore.at[c])
+        settle(out.at[0, pl.ds(0, count), :], semaphore.at[c])
 
     results = [
         pltpu.make_async_copy(value, target, o_sem.at[i])
@@ -468,17 +506,30 @@
     far_first(n, share_stress)
     for result in results[1:]:
         result.start()
-    for c in range(chunks):
-        guard(whole, mine, functools.partial(drain, c, nb * na - 1, d_send))
-        guard(whole, mine, functools.partial(drain, c, hb * ns - 1, g_send))
+    for m, (_, _, count) in enumerate(units):
+        guard(whole, mine, functools.partial(drain, m, (nb * na - 1) * count * zp, d_send))
         if not whole:
-            pl.when(s >= na)(functools.partial(drain, c, nb * na, d_send))
+            pl.when(s >= na)(functools.partial(drain, m, nb * na * count * zp, d_send))
+    for i in range(len(backs)):
+        guard(whole, mine, functools.partial(drain, i, (hb * ns - 1) * backs[i][3], g_send))
     settle(held, t_send.at[0])
     settle(held, t_recv.at[0])
     stress[...] = row[...] + jnp.sum(held[...], axis=0)
     results[0].start()
     for result in results:
         result.wait()
+
+
+def emit_kernel(stress, kdens, square, stress_o, kdens_o, square_o, semaphores):
+    copies = [
+        pltpu.make_async_copy(source, target, semaphores.at[i])
+        for i, (source, target) in enumerate(((square, square_o), (kdens, kdens_o)))
+    ]
+    for copy in copies:
+        copy.start()
+    stress_o[...] = stress[0, :6]
+    for copy in copies:
+        copy.wait()
 
 
 def params(number):
@@ -600,19 +651,28 @@
         + [
             dma(shape)
             for shape in (
-                (chunks,), (1,), (fold_y * ns - 1,), (fold_z // 2 - 1,), (1,),
-                (chunks,), (1,),
+                (chunks + 1,), (1,), (fold_y * ns - 1,), (fold_z // 2 - 1,), (1,),
+                (chunks + 2 if zl % 16 == 0 else chunks + 1,), (1,),
             )
             for _ in range(2)
         ],
         compiler_params=params(0),
         name="main_exchange",
     )(occupation, *fetched)
-    return (
-        stress[0, :6],
-        kinetic_density.reshape(rows * 128),
-        square[None],
-    )
+    anywhere = pl.BlockSpec(memory_space=pl.ANY)
+    resident = pl.BlockSpec(memory_space=pltpu.VMEM)
+    stress, kinetic_density, square = pl.pallas_call(
+        emit_kernel,
+        out_shape=[
+            jax.ShapeDtypeStruct(shape, jnp.float32) for shape in ((6,), (rows, 128), (zl, nx, ny))
+        ],
+        in_specs=[resident, anywhere, anywhere],
+        out_specs=[resident, anywhere, anywhere],
+        scratch_shapes=[dma((2,))],
+        compiler_params=pltpu.CompilerParams(vmem_limit_bytes=2**20),
+        name="emit",
+    )(stress, kinetic_density, square)
+    return stress, kinetic_density.reshape(rows * 128), square[None]
 
 
 def solution(mesh):

time: 73.5 us -> 69.1 us (0.940)
  Pallas kernels: 70.5 us -> 68.3 us
  local copies, waits for them, and re-layouts: 2.12 us -> 0 us
    pallas_call x1, Pallas kernels: 70.5 us -> 66.8 us  [shards(): pl.pallas_call(functools.partial(main_kernel, nb, ns, fold_y, fold_z), ou...]
    unnamed x2 -> x0, local copies, waits for them, and re-layouts: 1.6 us -> none
    pallas_call x0 -> x1, Pallas kernels: none -> 1.5 us  [shards(): pl.pallas_call(emit_kernel, out_shape=[jax.ShapeDtypeStruct(shape, jnp.fl...]
where the time goes in v4:
time: 69.1 us; the launch traced here: 68.9 us
  Pallas kernels  68.3 us (99%)
    pallas_call x1, Pallas kernels, shards(): pl.pallas_call(functools.partial(main_kernel, nb, ns, fold_y, fold_z), ou...  66.8 us
    pallas_call x1, Pallas kernels, shards(): pl.pallas_call(emit_kernel, out_shape=[jax.ShapeDtypeStruct(shape, jnp.fl...  1.5 us

profile of v4, /device:TPU:0, one launch (start us, length us, event | category | flops | bytes accessed | tf_op | source)
XLA Modules:
  0.0 68.9 jit_solution(11070525536496134083)
XLA Ops:
  0.6 66.8 %main_exchange.1 = (f32[1,128]{1,0:T(1,128)S(1)}, f32[128,128]{1,0:T(8,128)S(1)}, f32[16,128,128]{2,1,0:T(8,128)S(1)}) custom-call(s32[1,2]{1,0:T(1,128)} %occupation.1, f32[16,128,128]{2,1,0:T(8,128)} %bitcast.9, bf16[2,8192,128]{2,1,0:T(8,128)(2,1)} %bitcast.8, f32[2,256,8,128]{3,2,1,0:T(8,128)} %factor_h.1, bf16[4,64,256]{2,1,0:T(8,128)(2,1)} %constant.12.clone.table_f_h, ...), custom_call_target="tpu_custom_call" | custom-call | tf_op jit(solution)/shard_map/main_exchange/pallas_call | solution.py:613
  67.4 1.5 %emit.1 = (f32[6]{0:T(128)}, f32[128,128]{1,0:T(8,128)}, f32[16,128,128]{2,1,0:T(8,128)}) custom-call(f32[1,128]{1,0:T(1,128)S(1)} %get-tuple-element.9.stress, f32[128,128]{1,0:T(8,128)S(1)} %get-tuple-element.10.kdens, f32[16,128,128]{2,1,0:T(8,128)S(1)} %get-tuple-element.11.square), custom_call_target="tpu_custom_call" | custom-call | tf_op jit(solution)/shard_map/emit/pallas_call | solution.py:664

commit v5 on v4

--- a/solution.py
+++ b/solution.py
@@ -13,7 +13,7 @@
 spacing = 0.25
 MESH = pl.DeviceIdType.MESH
 CHUNKS = 4
-PLAN = (((0, 0), (1, 0)), ((0, 1), (0, 2), (0, 3), (0, 4), (1, 1), (1, 2)), ((1, 3), (1, 4)))
+PLAN = (((0, 0), (1, 0)), ((0, 1), (0, 2), (0, 3), (0, 4), (1, 1), (1, 2)), (), ((1, 3), (1, 4)))
 
 
 def derivative_table(length):
@@ -41,6 +41,11 @@
     loop(1, count // 2, step)
 
 
+def spread(count, step):
+    for k in (3, 1, 2, 0):
+        loop(max(k * count // 4, 1), (k + 1) * count // 4, step)
+
+
 def partner(b, s, offset, nb, ns):
     hop = lax.div(offset, ns)
     return wrapped(b + hop, nb), wrapped(s + offset - hop * ns, ns)
@@ -55,7 +60,7 @@
             barrier, inc=1, device_id=partner(b, s, k, nb, ns), device_id_type=MESH
         )
 
-    far_first(nb * ns, greet)
+    spread(nb * ns, greet)
     return b, s
 
 
@@ -114,12 +119,12 @@
 
 
 def main_kernel(
-    nb, ns, ny, nz, occupation, dens_h, coef_h, factor_h,
+    nb, ns, ny, nz, occupation_h, dens_h, coef_h, factor_h,
     table_f_h, table_i_h, table_y_h, table_d_h, table_z_h, table_g_h, miller_h,
-    stress_o, kdens_o, square_o,
-    dens, coef, factor, table_f, table_i, table_y, table_d, table_z, table_g, miller,
-    stress, kdens, square, squares, kin, out, col, grad, gout, from_core, sum_core, from_plane, sum_plane, from_line, pair, from_pair,
-    inverses, grad_x, grad_y, above, slopes, tally, part, row, held,
+    held, kdens_o, square_o,
+    occupation, dens, coef, factor, table_f, table_i, table_y, table_d, table_z, table_g, miller,
+    kdens, square, squares, kin, out, col, grad, gout, from_core, sum_core, from_plane, sum_plane, from_line, pair, from_pair,
+    inverses, grad_x, grad_y, above, below, flat, slopes, tally, part, row,
     f_sem, o_sem, d_send, d_recv, c_send, c_recv, p_send, p_recv, l_send, l_recv, x_send, x_recv,
     g_send, g_recv, t_send, t_recv,
 ):
@@ -156,6 +161,7 @@
     whole, mine = na == ns, s < na
     for fetch in fetches[:2]:
         fetch.wait()
+    fetches.append(pltpu.make_async_copy(occupation_h, occupation, f_sem.at[len(fetches)]))
     for fetch in fetches[2:]:
         fetch.start()
 
@@ -209,14 +215,14 @@
     pl.semaphore_wait(pltpu.get_barrier_semaphore(), n - 1)
     send_stage(0)
 
+    fetches[2].wait()
+    fetches[-1].wait()
     nbl = occupation.shape[1]
     depth = rows * nbl
     shares = [
         jnp.full((rows, 128), occupation[0, j]).astype(jnp.float32) / occupation_unit
         for j in range(nbl)
     ]
-    fetches[2].wait()
-
     def kinetic(i):
         for j in range(2):
             k = 2 * i + j
@@ -259,9 +265,12 @@
 
     def in_plane(i):
         value = split(dens[i])
-        grad_x[i] = dot3((table_g[0, 0], table_g[1, 0]), value)
-        grad_y[i] = dot3(value, (table_g[0, 1], table_g[1, 1]))
+        slope_x = dot3((table_g[0, 0], table_g[1, 0]), value)
+        slope_y = dot3(value, (table_g[0, 1], table_g[1, 1]))
+        grad_x[i], grad_y[i] = slope_x, slope_y
+        flat[i] = slope_x * slope_x + slope_y * slope_y
         scale = 4.0 * dens[i] * dens[i] + 1.0
+        below[i] = scale + flat[i]
         weigh = jnp.exp(jnp.log(dens[i]) * (-1.0 / 3.0)) * scale
         above[i] = weigh * (-1.0 / (nzg * nx * width))
 
@@ -460,10 +469,9 @@
             if chunks > 1:
                 here = here + slopes[spot]
             g = (grad_x[spot], grad_y[spot], here)
-            total = g[0] * g[0] + g[1] * g[1] + g[2] * g[2]
-            square[spot] = total
-            value = dens[spot]
-            weigh = above[spot] / (4.0 * value * value + 1.0 + total)
+            rise = here * here
+            square[spot] = flat[spot] + rise
+            weigh = above[spot] / (below[spot] + rise)
             scaled = [weigh * g[p] for p in range(3)]
             for t, (p, q) in enumerate(order):
                 term = (scaled[p] * g[q]).reshape(nx // 8, 8, width)
@@ -500,11 +508,12 @@
     results = [
         pltpu.make_async_copy(value, target, o_sem.at[i])
         for i, (value, target) in enumerate(
-            ((stress, stress_o), (kdens, kdens_o), (square, square_o))
+            ((kdens, kdens_o), (square, square_o))
         )
     ]
-    far_first(n, share_stress)
-    for result in results[1:]:
+    spread(n, share_stress)
+    pltpu.make_async_copy(row, held.at[n - 1], t_recv.at[0]).start()
+    for result in results:
         result.start()
     for m, (_, _, count) in enumerate(units):
         guard(whole, mine, functools.partial(drain, m, (nb * na - 1) * count * zp, d_send))
@@ -512,22 +521,26 @@
             pl.when(s >= na)(functools.partial(drain, m, nb * na * count * zp, d_send))
     for i in range(len(backs)):
         guard(whole, mine, functools.partial(drain, i, (hb * ns - 1) * backs[i][3], g_send))
-    settle(held, t_send.at[0])
-    settle(held, t_recv.at[0])
-    stress[...] = row[...] + jnp.sum(held[...], axis=0)
-    results[0].start()
+    settle(held.at[pl.ds(0, n - 1)], t_send.at[0])
     for result in results:
         result.wait()
-
-
-def emit_kernel(stress, kdens, square, stress_o, kdens_o, square_o, semaphores):
+    settle(held, t_recv.at[0])
+
+
+def emit_kernel(held, kdens, square, stress_o, kdens_o, square_o, semaphores):
+    step = max(square.shape[0] // 4, 1)
+    pieces = [
+        (square.at[pl.ds(i, step)], square_o.at[pl.ds(i, step)])
+        for i in range(0, square.shape[0], step)
+    ]
+    pieces.append((kdens, kdens_o))
     copies = [
         pltpu.make_async_copy(source, target, semaphores.at[i])
-        for i, (source, target) in enumerate(((square, square_o), (kdens, kdens_o)))
+        for i, (source, target) in enumerate(pieces)
     ]
     for copy in copies:
         copy.start()
-    stress_o[...] = stress[0, :6]
+    stress_o[...] = jnp.sum(held[...], axis=0)[0, :6]
     for copy in copies:
         copy.wait()
 
@@ -610,17 +623,16 @@
         miller,
     )
 
-    stress, kinetic_density, square = pl.pallas_call(
+    held, kinetic_density, square = pl.pallas_call(
         functools.partial(main_kernel, nb, ns, fold_y, fold_z),
-        out_shape=(vmem(1, 128), vmem(rows, 128), vmem(zl, nx, ny)),
-        in_specs=[pl.BlockSpec(memory_space=pltpu.SMEM)]
-        + [pl.BlockSpec(memory_space=pltpu.HBM)] * len(fetched),
+        out_shape=(vmem(nb * ns, 1, 128), vmem(rows, 128), vmem(zl, nx, ny)),
+        in_specs=[pl.BlockSpec(memory_space=pltpu.HBM)] * (len(fetched) + 1),
         out_specs=(pl.BlockSpec(memory_space=pl.ANY),) * 3,
-        scratch_shapes=[pltpu.VMEM(value.shape, value.dtype) for value in fetched]
+        scratch_shapes=[pltpu.SMEM(occupation.shape, occupation.dtype)]
+        + [pltpu.VMEM(value.shape, value.dtype) for value in fetched]
         + [
             pltpu.VMEM(shape, jnp.float32)
             for shape in (
-                (1, 128),
                 (rows, 128),
                 (zl, nx, ny),
                 (2, rows * nbl, 128),
@@ -641,13 +653,14 @@
                 (zl, nx, ny),
                 (zl, nx, ny),
                 (zl, nx, ny),
+                (zl, nx, ny),
+                (zl, nx, ny),
                 (6, 8, ny),
                 (8, 128),
                 (1, 128),
-                (nb * ns - 1, 1, 128),
             )
         ]
-        + [dma((len(fetched),)), dma((3,))]
+        + [dma((len(fetched) + 1,)), dma((2,))]
         + [
             dma(shape)
             for shape in (
@@ -668,10 +681,10 @@
         ],
         in_specs=[resident, anywhere, anywhere],
         out_specs=[resident, anywhere, anywhere],
-        scratch_shapes=[dma((2,))],
+        scratch_shapes=[dma((5,))],
         compiler_params=pltpu.CompilerParams(vmem_limit_bytes=2**20),
         name="emit",
-    )(stress, kinetic_density, square)
+    )(held, kinetic_density, square)
     return stress, kinetic_density.reshape(rows * 128), square[None]
 
 

time: 69.1 us -> 68.1 us (0.986)
  Pallas kernels: 68.3 us -> 67.3 us
    pallas_call x1, Pallas kernels: 66.8 us -> 65.8 us  [shards(): pl.pallas_call(functools.partial(main_kernel, nb, ns, fold_y, fold_z), ou...]
where the time goes in v5:
time: 68.1 us; the launch traced here: 68 us
  Pallas kernels  67.3 us (99%)
    pallas_call x1, Pallas kernels, shards(): pl.pallas_call(functools.partial(main_kernel, nb, ns, fold_y, fold_z), ou...  65.8 us
    pallas_call x1, Pallas kernels, shards(): pl.pallas_call(emit_kernel, out_shape=[jax.ShapeDtypeStruct(shape, jnp.fl...  1.53 us

profile of v5, /device:TPU:0, one launch (start us, length us, event | category | flops | bytes accessed | tf_op | source)
XLA Modules:
  0.0 68.0 jit_solution(3805919299657079796)
XLA Ops:
  0.6 65.8 %main_exchange.1 = (f32[32,1,128]{2,1,0:T(1,128)S(1)}, f32[128,128]{1,0:T(8,128)S(1)}, f32[16,128,128]{2,1,0:T(8,128)S(1)}) custom-call(s32[1,2]{1,0:T(1,128)} %occupation_h.1, f32[16,128,128]{2,1,0:T(8,128)} %bitcast.9, bf16[2,8192,128]{2,1,0:T(8,128)(2,1)} %bitcast.8, f32[2,256,8,128]{3,2,1,0:T(8,128)} %factor_h.1, ...), custom_call_target="tpu_custom_call" | custom-call | tf_op jit(solution)/shard_map/main_exchange/pallas_call | solution.py:626
  66.4 1.5 %emit.1 = (f32[6]{0:T(128)}, f32[128,128]{1,0:T(8,128)}, f32[16,128,128]{2,1,0:T(8,128)}) custom-call(f32[32,1,128]{2,1,0:T(1,128)S(1)} %get-tuple-element.9.held, f32[128,128]{1,0:T(8,128)S(1)} %get-tuple-element.10.kdens, f32[16,128,128]{2,1,0:T(8,128)S(1)} %get-tuple-element.11.square), custom_call_target="tpu_custom_call" | custom-call | tf_op jit(solution)/shard_map/emit/pallas_call | solution.py:677

commit v6 on v5

--- a/solution.py
+++ b/solution.py
@@ -172,7 +172,7 @@
         at = pl.multiple_of((tb * na + ts) * block + r * zp, 8)
         return ts < na, pltpu.make_async_remote_copy(
             out.at[c, pl.ds(at, count * zp), :], col.at[c, s, b, pl.ds(r * zp, count * zp), :],
-            d_send.at[m], d_recv.at[m], device_id=(tb, ts), device_id_type=MESH,
+            d_send.at[0], d_recv.at[m], device_id=(tb, ts), device_id_type=MESH,
         )
 
     def forward(i, which):
@@ -302,7 +302,7 @@
         at = pl.multiple_of(((c * hb + u) * na + s) * block + edge, 8)
         return pltpu.make_async_remote_copy(
             grad.at[c, ts, tu, pl.ds(edge, count), :], gout.at[pl.ds(at, count), :],
-            g_send.at[i], g_recv.at[i], device_id=(half * hb + tu, ts), device_id_type=MESH,
+            g_send.at[0], g_recv.at[i], device_id=(half * hb + tu, ts), device_id_type=MESH,
         )
 
     def local_back(i):
@@ -390,7 +390,7 @@
                 spot = pl.ds(pl.multiple_of(r * zp, zp), zl)
                 grad[c, k, :, spot, :] = slope[:, k * width:(k + 1) * width].reshape(hb, zl, width)
 
-        def transform(i):
+        def transform(c, i):
             j = c * each + i
             real, imag = column(c, 0, i), column(c, 0, each + i)
             for k in range(1, ns):
@@ -432,19 +432,23 @@
                     far_first(hb * ns, lambda k: back_copy(i, k).start())
                     local_back(i)
 
-        def spectrum():
-            loop(0, each, transform)
+        spectrum = functools.partial(loop, 0, each, functools.partial(transform, c))
 
         guard(whole, mine, work)
         if m == max(chunks - 3, 0):
             finish_planes()
         send_stage(m + 2)
-        if start + count == rc:
+        later = chunks > 2 and m == chunks - 2
+        if later:
+            postponed = spectrum
+        elif start + count == rc:
             guard(whole, mine, spectrum)
         if m == max(chunks - 2, 0):
             cross_lines()
-        done = m - 2 if start else m - 1
-        if 0 <= done and m != chunks - 1:
+        done = m - 2 if chunks > 2 and m >= chunks - 1 or start else m - 1
+        if chunks > 2 and m == chunks - 1:
+            guard(whole, mine, postponed)
+        if 0 <= done and not later and (chunks > 2 or m != chunks - 1):
             gather_back(done)
             loop(0, zl // 2, functools.partial(invert_chunk, done))
 
@@ -502,8 +506,8 @@
     def share_stress(k):
         stress_copy(k).start()
 
-    def drain(c, count, semaphore):
-        settle(out.at[0, pl.ds(0, count), :], semaphore.at[c])
+    def drain(count, semaphore):
+        settle(out.at[:, pl.ds(0, count * block), :], semaphore.at[0])
 
     results = [
         pltpu.make_async_copy(value, target, o_sem.at[i])
@@ -515,12 +519,10 @@
     pltpu.make_async_copy(row, held.at[n - 1], t_recv.at[0]).start()
     for result in results:
         result.start()
-    for m, (_, _, count) in enumerate(units):
-        guard(whole, mine, functools.partial(drain, m, (nb * na - 1) * count * zp, d_send))
-        if not whole:
-            pl.when(s >= na)(functools.partial(drain, m, nb * na * count * zp, d_send))
-    for i in range(len(backs)):
-        guard(whole, mine, functools.partial(drain, i, (hb * ns - 1) * backs[i][3], g_send))
+    guard(whole, mine, functools.partial(drain, nb * na - 1, d_send))
+    if not whole:
+        pl.when(s >= na)(functools.partial(drain, nb * na, d_send))
+    guard(whole, mine, functools.partial(drain, hb * ns - 1, g_send))
     settle(held.at[pl.ds(0, n - 1)], t_send.at[0])
     for result in results:
         result.wait()
@@ -662,12 +664,12 @@
         ]
         + [dma((len(fetched) + 1,)), dma((2,))]
         + [
-            dma(shape)
-            for shape in (
-                (chunks + 1,), (1,), (fold_y * ns - 1,), (fold_z // 2 - 1,), (1,),
-                (chunks + 2 if zl % 16 == 0 else chunks + 1,), (1,),
+            dma((count,))
+            for pair in (
+                (1, chunks + 1), (1, 1), (fold_y * ns - 1,) * 2, (fold_z // 2 - 1,) * 2, (1, 1),
+                (1, chunks + 2 if zl % 16 == 0 else chunks + 1), (1, 1),
             )
-            for _ in range(2)
+            for count in pair
         ],
         compiler_params=params(0),
         name="main_exchange",

time: 68.1 us -> 68 us (level)
  no operation moved by 1% of the time
where the time goes in v6:
time: 68 us; the launch traced here: 67.9 us
  Pallas kernels  67.3 us (99%)
    pallas_call x1, Pallas kernels, shards(): pl.pallas_call(functools.partial(main_kernel, nb, ns, fold_y, fold_z), ou...  65.7 us
    pallas_call x1, Pallas kernels, shards(): pl.pallas_call(emit_kernel, out_shape=[jax.ShapeDtypeStruct(shape, jnp.fl...  1.53 us

profile of v6, /device:TPU:0, one launch (start us, length us, event | category | flops | bytes accessed | tf_op | source)
XLA Modules:
  0.0 67.9 jit_solution(1636917398619909556)
XLA Ops:
  0.6 65.7 %main_exchange.1 = (f32[32,1,128]{2,1,0:T(1,128)S(1)}, f32[128,128]{1,0:T(8,128)S(1)}, f32[16,128,128]{2,1,0:T(8,128)S(1)}) custom-call(s32[1,2]{1,0:T(1,128)} %occupation_h.1, f32[16,128,128]{2,1,0:T(8,128)} %bitcast.9, bf16[2,8192,128]{2,1,0:T(8,128)(2,1)} %bitcast.8, f32[2,256,8,128]{3,2,1,0:T(8,128)} %factor_h.1, ...), custom_call_target="tpu_custom_call" | custom-call | tf_op jit(solution)/shard_map/main_exchange/pallas_call | solution.py:628
  66.4 1.5 %emit.1 = (f32[6]{0:T(128)}, f32[128,128]{1,0:T(8,128)}, f32[16,128,128]{2,1,0:T(8,128)}) custom-call(f32[32,1,128]{2,1,0:T(1,128)S(1)} %get-tuple-element.9.held, f32[128,128]{1,0:T(8,128)S(1)} %get-tuple-element.10.kdens, f32[16,128,128]{2,1,0:T(8,128)S(1)} %get-tuple-element.11.square), custom_call_target="tpu_custom_call" | custom-call | tf_op jit(solution)/shard_map/emit/pallas_call | solution.py:679
